TPU v7x, 16 devices: a whole 2x2x2 slice. The times are simulated.
16 devices in a mesh: dp: 4 (over z, y), tp: 4 (over x, core).
Axes of the slice: x: 2, y: 2, z: 2, core: 2. Of those that a mesh axis runs over, the one named last changes fastest.
Arguments:
- x_norm: bfloat16 [8192, 2048], P(('dp', 'tp')), parts along dimension 0
- grad_y: bfloat16 [8192, 2048], P(('dp', 'tp')), parts along dimension 0
- u_gate: bfloat16 [8192, 8192], P('dp', 'tp'), parts along dimension 0
- u_up: bfloat16 [8192, 8192], P('dp', 'tp'), parts along dimension 0
- w_gate: bfloat16 [2048, 8192], P(None, 'tp')
- w_up: bfloat16 [2048, 8192], P(None, 'tp')
- w_down: bfloat16 [8192, 2048], P('tp')
- x_in: bfloat16 [8192, 2048], P(('dp', 'tp')), parts along dimension 0
- gamma: bfloat16 [2048], replicated
- grad_res: bfloat16 [8192, 2048], P(('dp', 'tp')), parts along dimension 0
- attn_out: bfloat16 [8192, 2048], P('dp', 'tp'), parts along dimension 0
- w_out: bfloat16 [2048, 2048], P('tp')
Outputs:
- output 1: bfloat16 [8192, 2048], P(('dp', 'tp')), parts along dimension 0
- output 2: bfloat16 [8192, 2048], P('dp', 'tp'), parts along dimension 0
- output 3: float32 [8192, 8192], P('dp', 'tp'), parts along dimension 0
- output 4: float32 [8192, 8192], P('dp', 'tp'), parts along dimension 0
- output 5: float32 [32768, 2048], P(('dp', 'tp')), parts along dimension 0
- output 6: float32 [8192, 2048], P(('dp', 'tp')), parts along dimension 0
There are 4 independent parts. A program takes and returns all parts, laid end to end along the dimension named above; an argument that names none is the same for every part.
All inputs are finite; a program needn't handle non-finite values.
Results may differ from a plain program's by a relative error of at most 0.0124612.
Values are sent between devices in bfloat16 or wider.
A program may use at most 1 GiB of HBM per device.

v0:
```python
import jax
import jax.numpy as jnp
from jax import lax
from jax.sharding import PartitionSpec as P

NORM_EPS = 1e-5
CONTRACT_ROWS = (((0,), (0,)), ((), ()))
CONTRACT_COLS = (((1,), (1,)), ((), ()))


def rms_backward(grad_x, x_in, gamma, grad_res):
    xin_f = x_in.astype(jnp.float32)
    inv_rms = lax.rsqrt(jnp.mean(xin_f * xin_f, axis=-1, keepdims=True) + NORM_EPS)
    scaled = grad_x.astype(jnp.float32) * gamma.astype(jnp.float32)
    proj_mean = jnp.mean(scaled * xin_f, axis=-1, keepdims=True)
    return (grad_res.astype(jnp.float32)
            + inv_rms * (scaled - xin_f * (inv_rms * inv_rms) * proj_mean)).astype(jnp.bfloat16)


def solution(mesh):
    token_spec = P(("dp", "tp"), None)
    split_cols = P("dp", "tp")
    weight_cols = P(None, "tp")
    weight_rows = P("tp", None)

    def local_backward(x_norm, grad_y, u_gate, u_up, w_gate, w_up, w_down, x_in, gamma, grad_res, attn_out, w_out):
        x_full = lax.all_gather(x_norm, "tp", axis=0, tiled=True)
        gy_full = lax.all_gather(grad_y, "tp", axis=0, tiled=True)
        gate_f = u_gate.astype(jnp.float32)
        up_f = u_up.astype(jnp.float32)
        sig_gate = jax.nn.sigmoid(gate_f)
        act_gate = gate_f * sig_gate
        silu_grad = sig_gate * (1.0 + gate_f * (1.0 - sig_gate))
        hidden_z = (act_gate * up_f).astype(jnp.bfloat16)
        gw_down = lax.dot_general(hidden_z, gy_full, CONTRACT_ROWS, preferred_element_type=jnp.float32)
        grad_h = lax.dot_general(gy_full, w_down, CONTRACT_COLS, preferred_element_type=jnp.float32)
        grad_up = (grad_h * act_gate).astype(jnp.bfloat16)
        grad_gate = (grad_h * up_f * silu_grad).astype(jnp.bfloat16)
        part_x = (lax.dot_general(grad_gate, w_gate, CONTRACT_COLS, preferred_element_type=jnp.float32)
                  + lax.dot_general(grad_up, w_up, CONTRACT_COLS, preferred_element_type=jnp.float32))
        grad_x = lax.psum_scatter(part_x.astype(jnp.bfloat16), "tp", scatter_dimension=0, tiled=True)
        gw_gate = lax.dot_general(x_full, grad_gate, CONTRACT_ROWS, preferred_element_type=jnp.float32)
        gw_up = lax.dot_general(x_full, grad_up, CONTRACT_ROWS, preferred_element_type=jnp.float32)
        grad_sum = rms_backward(grad_x, x_in, gamma, grad_res)
        gs_full = lax.all_gather(grad_sum, "tp", axis=0, tiled=True)
        grad_attn = lax.dot_general(gs_full, w_out, CONTRACT_COLS, preferred_element_type=jnp.float32).astype(jnp.bfloat16)
        gw_out = lax.dot_general(attn_out, gs_full, CONTRACT_ROWS, preferred_element_type=jnp.float32)
        return grad_sum, grad_attn, gw_gate, gw_up, gw_down, gw_out

    return jax.shard_map(
        local_backward,
        mesh=mesh,
        in_specs=(token_spec, token_spec, split_cols, split_cols, weight_cols, weight_cols, weight_rows,
                  token_spec, P(None), token_spec, split_cols, weight_rows),
        out_specs=(token_spec, split_cols, split_cols, split_cols, token_spec, token_spec),
        check_vma=False,
    )
```

profile of v0, /device:TPU:0, one launch (start us, length us, event | category | flops | bytes accessed | tf_op | source)
XLA Modules:
  0.0 421.4 jit_solution(7803082795229791734)
XLA Ops:
  7.2 0.0 copy-start
  7.2 0.0 all-gather.4.cloned.1.call-start
  7.2 0.7 all-gather.4.cloned.1.call-update
  7.9 0.0 reduce-scatter.2.cloned.1.call-start
  8.0 61.1 %all-gather.4.cloned.1.call-done = bf16[2048,2048]{1,0:T(8,128)(2,1)} async-done(((bf16[512,2048]{1,0:T(8,128)(2,1)}), bf16[2048,2048]{1,0:T(8,128)(2,1)}) %all-gather.4.cloned.1.call-update) | async-done | bytes 8388624 | tf_op jit(solution)/shard_map/all_gather | solution.py:28
  69.0 31.5 %fusion.1 = (bf16[2048,2048]{1,0:T(8,128)(2,1)}, f32[2048,2048]{1,0:T(8,128)}) fusion(bf16[2048,2048]{1,0:T(8,128)(2,1)} %param.15, bf16[2048,2048]{1,0:T(8,128)(2,1)} %param.14, bf16[2048,2048]{1,0:T(8,128)(2,1)} %all-gather.4.cloned.1.call-done, bf16[2048,2048]{1,0:T(8,128)(2,1)} %param.18), kind=kOutput, calls=%fused_computation.6 | convolution fusion | flops 17230200832 | bytes 58720256 | tf_op jit(solution)/shard_map/dot_general | solution.py:36
  100.5 24.3 %fusion.19 = f32[2048,2048]{1,0:T(8,128)} fusion(bf16[2048,2048]{1,0:T(8,128)(2,1)} %get-tuple-element.16, bf16[2048,2048]{1,0:T(8,128)(2,1)} %param.16), kind=kOutput, calls=%fused_computation.35 | convolution fusion | flops 17179869184 | bytes 33554432 | tf_op jit(solution)/shard_map/dot_general | solution.py:39
  124.9 27.3 %add_convert_fusion = bf16[2048,2048]{1,0:T(8,128)(2,1)} fusion(f32[2048,2048]{1,0:T(8,128)} %fusion.19, bf16[2048,2048]{1,0:T(8,128)(2,1)} %param.17, f32[2048,2048]{1,0:T(8,128)} %get-tuple-element.17, bf16[2048,2048]{1,0:T(8,128)(2,1)} %param.14), kind=kOutput, calls=%fused_computation.13 | convolution fusion | flops 17217617920 | bytes 58720256 | tf_op jit(solution)/shard_map/dot_general | solution.py:40
  152.2 0.0 copy-start.1
  152.2 0.0 reduce-scatter.2.cloned.1.call-update
  152.2 0.0 all-gather.8.cloned.1.call-start
  152.3 0.7 all-gather.8.cloned.1.call-update
  153.0 0.0 all-gather.6.cloned.1.call-start
  153.0 0.0 copy-done.1
  153.1 66.2 %reduce-scatter.2.cloned.1.call-done = bf16[512,2048]{1,0:T(8,128)(2,1)} async-done(((bf16[2048,2048]{1,0:T(8,128)(2,1)}), bf16[512,2048]{1,0:T(8,128)(2,1)}) %reduce-scatter.2.cloned.1.call-update) | async-done | bytes 2097168 | tf_op jit(solution)/shard_map/reduce_scatter | solution.py:41
  219.3 3.3 fusion.10
  222.6 5.7 %fusion.15 = bf16[512,2048]{1,0:T(8,128)(2,1)} fusion(bf16[512,2048]{1,0:T(8,128)(2,1)} %param.19, bf16[512,2048]{1,0:T(8,128)(2,1)} %reduce-scatter.2.cloned.1.call-done, bf16[512,2048]{1,0:T(8,128)(2,1)} %param.21, f32[512]{0:T(512)S(1)} %broadcast_multiply_fusion, f32[512]{0:T(512)S(1)} %get-tuple-element.15, f32[2048]{0:T(1024)S(1)} %convert_element_type.44, ...), kind=kLoop, calls=%fused_computation.26 | loop fusion | flops 10485760 | bytes 8402944 | tf_op jit(solution)/shard_map/convert_element_type | solution.py:17
  228.3 0.0 all-gather.6.cloned.1.call-update
  228.3 49.2 %all-gather.8.cloned.1.call-done = bf16[2048,2048]{1,0:T(8,128)(2,1)} async-done(((bf16[512,2048]{1,0:T(8,128)(2,1)}), bf16[2048,2048]{1,0:T(8,128)(2,1)}) %all-gather.8.cloned.1.call-update) | async-done | bytes 8388624 | tf_op jit(solution)/shard_map/all_gather | solution.py:27
  277.5 24.6 %convolution_bitcast_fusion.1 = f32[2048,2048]{0,1:T(8,128)} fusion(bf16[2048,2048]{1,0:T(8,128)(2,1)} %get-tuple-element.16, bf16[2048,2048]{1,0:T(8,128)(2,1)} %all-gather.8.cloned.1.call-done), kind=kOutput, calls=%fused_computation.16 | convolution fusion | flops 17179869184 | bytes 33554432 | tf_op jit(solution)/shard_map/dot_general | solution.py:42
  302.1 17.6 %copy.18 = f32[2048,2048]{1,0:T(8,128)} copy(f32[2048,2048]{0,1:T(8,128)} %convolution_bitcast_fusion.1) | data formatting | bytes 33554432
  319.7 26.2 %convolution_bitcast_fusion = f32[2048,2048]{0,1:T(8,128)} fusion(bf16[2048,2048]{1,0:T(8,128)(2,1)} %all-gather.8.cloned.1.call-done, f32[2048,2048]{1,0:T(8,128)} %get-tuple-element.17, bf16[2048,2048]{1,0:T(8,128)(2,1)} %param.14), kind=kOutput, calls=%fused_computation.15 | convolution fusion | flops 17209229312 | bytes 50331648 | tf_op jit(solution)/shard_map/dot_general | solution.py:43
  345.8 17.6 %copy.19 = f32[2048,2048]{1,0:T(8,128)} copy(f32[2048,2048]{0,1:T(8,128)} %convolution_bitcast_fusion) | data formatting | bytes 33554432
  363.4 26.0 %fusion.8 = f32[2048,2048]{1,0:T(8,128)} fusion(bf16[2048,2048]{1,0:T(8,128)(2,1)} %all-gather.4.cloned.1.call-done, bf16[2048,2048]{1,0:T(8,128)(2,1)} %param.15, bf16[2048,2048]{1,0:T(8,128)(2,1)} %param.14), kind=kOutput, calls=%fused_computation.17 | convolution fusion | flops 17213423616 | bytes 41943040 | tf_op jit(solution)/shard_map/dot_general | solution.py:35
  389.4 0.0 all-gather.6.cloned.1.call-done
  389.4 0.0 copy-done
  389.4 9.8 %convolution_bitcast_fusion.2 = f32[512,2048]{0,1:T(8,128)} fusion(bf16[2048,2048]{1,0:T(8,128)(2,1)} %all-gather.6.cloned.1.call-done, bf16[2048,512]{1,0:T(8,128)(2,1)S(1)} %copy-done), kind=kOutput, calls=%fused_computation.29 | convolution fusion | flops 4294967296 | bytes 14680064 | tf_op jit(solution)/shard_map/dot_general | solution.py:47
  399.2 5.3 %copy.20 = f32[512,2048]{1,0:T(8,128)} copy(f32[512,2048]{0,1:T(8,128)} %convolution_bitcast_fusion.2) | data formatting | bytes 8388608
  404.6 9.9 %convolution_convert_fusion = bf16[2048,512]{1,0:T(8,128)(2,1)} fusion(bf16[2048,2048]{1,0:T(8,128)(2,1)} %all-gather.6.cloned.1.call-done, bf16[512,2048]{1,0:T(8,128)(2,1)} %param.23), kind=kOutput, calls=%fused_computation.30 | convolution fusion | flops 4296015872 | bytes 12582912 | tf_op jit(solution)/shard_map/dot_general | solution.py:46
  (3 shorter events, 0.0 us)
Async XLA Ops:
  7.2 382.2 %copy-start = (bf16[2048,512]{1,0:T(8,128)(2,1)S(1)}, bf16[2048,512]{1,0:T(8,128)(2,1)}, u32[]{:S(2)}) copy-start(bf16[2048,512]{1,0:T(8,128)(2,1)} %param.22) | copy-start | bytes 6291460
  7.2 61.8 %all-gather.4.cloned.1.call-start = ((), (), s32[]{:S(2)}) async-start(), calls=%async_computation.1 | async-start | bytes 10485760 | tf_op jit(solution)/shard_map/all_gather | solution.py:28
  7.9 211.4 %reduce-scatter.2.cloned.1.call-start = ((), (), s32[]{:S(2)}) async-start(), calls=%async_computation.2 | async-start | bytes 10485760 | tf_op jit(solution)/shard_map/reduce_scatter | solution.py:41
  152.2 0.8 copy-start.1
  152.2 125.3 %all-gather.8.cloned.1.call-start = ((), (), s32[]{:S(2)}) async-start(), calls=%async_computation.4 | async-start | bytes 10485760 | tf_op jit(solution)/shard_map/all_gather | solution.py:27
  153.0 236.4 %all-gather.6.cloned.1.call-start = ((), (), s32[]{:S(2)}) async-start(), calls=%async_computation.3 | async-start | bytes 10485760 | tf_op jit(solution)/shard_map/all_gather | solution.py:45
Sparse Core Ops, SparseCore 0:
  9.5 59.4 all-gather.3
  152.4 66.8 reduce-scatter.1
  220.8 56.6 all-gather.7
  279.5 56.6 all-gather.5
where the time goes:
time: 430 us; the launch traced here: 421 us
  matrix products  180 us (42%)
  waiting for transfers between devices  178 us (41%)
  local copies, waits for them, and re-layouts  40.5 us (9%)
  between operations  14.2 us (3%)
  other arithmetic  8.98 us (2%)
    reduce_scatter x1, waiting for transfers between devices, local_backward(): lax.psum_scatter(part_x.astype(jnp.bfloat16), 'tp', scatter_dimension=0,...  66.2 us
    all_gather x1, waiting for transfers between devices, local_backward(): gy_full = lax.all_gather(grad_y, 'tp', axis=0, tiled=True)  61.1 us
    all_gather x1, waiting for transfers between devices, local_backward(): x_full = lax.all_gather(x_norm, 'tp', axis=0, tiled=True)  49.2 us
    unnamed x7, local copies, waits for them, and re-layouts  40.5 us
    dot_general x1, matrix products, local_backward(): lax.dot_general(gy_full, w_down, CONTRACT_COLS, preferred_element_type=jn...  31.5 us
    dot_general x1, matrix products, local_backward(): lax.dot_general(grad_up, w_up, CONTRACT_COLS, preferred_element_type=jnp....  27.3 us
    dot_general x1, matrix products, local_backward(): lax.dot_general(x_full, grad_up, CONTRACT_ROWS, preferred_element_type=jn...  26.2 us
    dot_general x1, matrix products, local_backward(): lax.dot_general(hidden_z, gy_full, CONTRACT_ROWS, preferred_element_type=...  26 us
  transfers between devices with their start and end apart: 4, of which 3 were waited for; matrix products, arithmetic and copies ran while one was open for 29% of the time, Pallas kernels for 0%

commit v1 on v0

v1 whole, which is shorter than its diff:
```python
import functools

import jax
import jax.numpy as jnp
from jax import lax
from jax.experimental import pallas as pl
from jax.experimental.pallas import tpu as pltpu
from jax.sharding import PartitionSpec as P


F32 = jnp.float32
BF16 = jnp.bfloat16
NORM_EPS = 1e-5
ROWS_T = (((0,), (0,)), ((), ()))
COLS_T = (((1,), (1,)), ((), ()))
ANY = pl.BlockSpec(memory_space=pl.ANY)
VMEM_LIMIT = 60 * 1024 * 1024
BLOCK = 512

CROSS = [(0, 2), (2, 0), (1, 3), (3, 1)]
PAIR = [(0, 1), (1, 0), (2, 3), (3, 2)]
OWN, SIB, FAR, DIAG = 0, 1, 2, 3


def dot(a, b, dims):
    return lax.dot_general(a, b, dims, preferred_element_type=F32)


def block_of(k):
    return lax.axis_index("tp") ^ k


def params(limit=VMEM_LIMIT):
    return pltpu.CompilerParams(vmem_limit_bytes=limit)


def hbm(*arrays):
    return [pltpu.with_memory_space_constraint(a, pltpu.HBM) for a in arrays]


def once(shape, index=None):
    return pl.BlockSpec(shape, index or (lambda *_: (0,) * len(shape)), pipeline_mode=pl.Buffered(1))


def hidden_body(n, tiles, *refs):
    dys, ugs, uus = refs[:n], refs[n:2 * n], refs[2 * n:3 * n]
    wd, wg, wu = refs[3 * n:3 * n + 3]
    dg, du, z = refs[-(n + 6):-(n + 3)]
    ps, (acc, held_g, held_u) = refs[-(n + 3):-3], refs[-3:]
    step = pl.program_id(0)
    rows = dys[0].shape[0]

    def form(slot):
        for i in range(n):
            span = pl.ds(i * rows, rows)
            grad_h = dot(dys[i][...], wd[...], COLS_T)
            gate = ugs[i][...].astype(F32)
            up = uus[i][...].astype(F32)
            sig = jax.nn.sigmoid(gate)
            act = gate * sig
            z[span, :] = (act * up).astype(BF16)
            grad_up = (grad_h * act).astype(BF16)
            grad_gate = (grad_h * up * (sig * (1.0 + gate * (1.0 - sig)))).astype(BF16)
            du[span, :] = grad_up
            dg[span, :] = grad_gate
            held_u[slot, span, :] = grad_up
            held_g[slot, span, :] = grad_gate

    def term(slot):
        return dot(held_g[slot], wg[...], COLS_T) + dot(held_u[slot], wu[...], COLS_T)

    @pl.when(step == 0)
    def _():
        acc[...] = jnp.zeros_like(acc)
        form(0)

    @pl.when((step > 0) & (step < tiles))
    def _():
        slot = lax.rem(step, 2)
        acc[...] += term(1 - slot)
        form(slot)

    @pl.when(step == tiles)
    def _():
        total = acc[...] + term((tiles - 1) % 2)
        for i in range(n):
            ps[i][...] = total[i * rows:(i + 1) * rows].astype(BF16)


def hidden(blocks, dys, start, rows, u_gate, u_up, w_down, w_gate, w_up, deps=(), tile=512):
    n = len(blocks)
    width = dys[0].shape[1]
    cols = w_down.shape[0]
    tiles = cols // tile
    per, first = BLOCK // rows, start // rows
    now = lambda s: jnp.minimum(s, tiles - 1)
    before = lambda s: jnp.maximum(s - 1, 0)
    u_specs = [pl.BlockSpec((rows, tile), functools.partial(lambda k, s: (block_of(k) * per + first, now(s)), k)) for k in blocks]
    tile_out = pl.BlockSpec((n * rows, tile), lambda s: (0, now(s)))
    w_late = pl.BlockSpec((width, tile), lambda s: (0, before(s)))
    return pl.pallas_call(
        functools.partial(hidden_body, n, tiles),
        grid=(tiles + 1,),
        in_specs=[once((rows, width), lambda s: (first, 0))] * n + u_specs + u_specs
        + [pl.BlockSpec((tile, width), lambda s: (now(s), 0)), w_late, w_late] + [ANY] * len(deps),
        out_specs=[tile_out] * 3 + [once((rows, width))] * n,
        out_shape=[jax.ShapeDtypeStruct((n * rows, cols), BF16)] * 3 + [jax.ShapeDtypeStruct((rows, width), BF16)] * n,
        scratch_shapes=[pltpu.VMEM((n * rows, width), F32)] + [pltpu.VMEM((2, n * rows, tile), BF16)] * 2,
        compiler_params=params(),
        cost_estimate=pl.CostEstimate(flops=6 * n * rows * width * cols, bytes_accessed=50 << 20, transcendentals=n * rows * cols),
    )(*hbm(*dys, *([u_gate] * n), *([u_up] * n), w_down, w_gate, w_up, *deps))


def grad_body(n, *refs):
    lefts, rights, out = refs[:n], refs[n:2 * n], refs[-1]
    total = dot(lefts[0][...], rights[0][...], ROWS_T)
    for a, b in zip(lefts[1:], rights[1:]):
        total += dot(a[...], b[...], ROWS_T)
    out[...] = total


def weight_grad(lefts, rights, deps=(), tm=256, tn=2048):
    n = len(lefts)
    m, cols = lefts[0][0].shape[1], rights[0][0].shape[1]
    l_specs = [pl.BlockSpec((r, tm), functools.partial(lambda b, j, i: (b, i), s // r)) for _, s, r in lefts]
    r_specs = [(pl.BlockSpec if tn < cols else once)((r, tn), functools.partial(lambda b, j, i: (b, j), s // r)) for _, s, r in rights]
    tokens = sum(r for _, _, r in lefts)
    return pl.pallas_call(
        functools.partial(grad_body, n),
        grid=(cols // tn, m // tm),
        in_specs=l_specs + r_specs + [ANY] * len(deps),
        out_specs=pl.BlockSpec((tm, tn), lambda j, i: (i, j)),
        out_shape=jax.ShapeDtypeStruct((m, cols), F32),
        compiler_params=params(),
        cost_estimate=pl.CostEstimate(flops=2 * tokens * m * cols, bytes_accessed=32 << 20, transcendentals=0),
    )(*hbm(*[a for a, _, _ in lefts], *[a for a, _, _ in rights], *deps))


def add_body(a, b, *refs):
    refs[-1][...] = (a[...].astype(F32) + b[...].astype(F32)).astype(BF16)


def add(a, b, tile=64):
    rows, width = a.shape
    spec = pl.BlockSpec((tile, width), lambda i: (i, 0))
    return pl.pallas_call(
        add_body,
        grid=(rows // tile,),
        in_specs=[spec, spec],
        out_specs=spec,
        out_shape=jax.ShapeDtypeStruct((rows, width), BF16),
        compiler_params=params(24 << 20),
        cost_estimate=pl.CostEstimate(flops=1000 * rows * width, bytes_accessed=6 * rows * width, transcendentals=0),
    )(*hbm(a, b))


def norm_body(p_own, p_pair, p_far, x_in, grad_res, gamma, *refs):
    piece, whole = refs[-2:]
    grad_x = (p_own[...].astype(F32) + p_pair[...].astype(F32) + p_far[...].astype(F32)).astype(BF16)
    xin = x_in[...].astype(F32)
    inv = lax.rsqrt(jnp.mean(xin * xin, axis=-1, keepdims=True) + NORM_EPS)
    scaled = grad_x.astype(F32) * gamma[...].astype(F32)
    proj = jnp.mean(scaled * xin, axis=-1, keepdims=True)
    res = (grad_res[...].astype(F32) + inv * (scaled - xin * (inv * inv) * proj)).astype(BF16)
    piece[...] = res
    whole[...] = res


def norm_backward(start, p_own, p_pair, p_far, x_in, grad_res, gamma, prev, deps=(), tile=64):
    rows, width = p_far.shape
    first = start // tile
    here = pl.BlockSpec((tile, width), lambda i: (first + i, 0))
    part = pl.BlockSpec((tile, width), lambda i: (i, 0))
    extra = ([] if prev is None else [prev]) + list(deps)
    return pl.pallas_call(
        norm_body,
        grid=(rows // tile,),
        in_specs=[here, here, part, here, here, once((1, width))] + [ANY] * len(extra),
        out_specs=[part, here],
        out_shape=[jax.ShapeDtypeStruct((rows, width), BF16), jax.ShapeDtypeStruct(p_own.shape, BF16)],
        input_output_aliases={} if prev is None else {6: 1},
        compiler_params=params(24 << 20),
        cost_estimate=pl.CostEstimate(flops=2000 * rows * width, bytes_accessed=14 * rows * width, transcendentals=0),
    )(*hbm(p_own, p_pair, p_far, x_in, grad_res, gamma, *extra))


def proj_body(blocks, start, first, *refs):
    ds0, ds1, o0, o1, w_out = refs[:5]
    prev_w = None if first else refs[5]
    grad_o, grad_w, acc, stage, sem = refs[-5:]
    step = pl.program_id(0)
    rows = ds0.shape[0]

    @pl.when(step == 0)
    def _():
        acc[...] = jnp.zeros_like(acc)

    acc[pl.ds(0, rows), :] += dot(ds0[...], w_out[...], COLS_T)
    acc[pl.ds(rows, rows), :] += dot(ds1[...], w_out[...], COLS_T)
    total = dot(o0[...], ds0[...], ROWS_T) + dot(o1[...], ds1[...], ROWS_T)
    grad_w[...] = total if first else prev_w[...] + total

    @pl.when(step == pl.num_programs(0) - 1)
    def _():
        stage[...] = acc[...].astype(BF16)
        copies = [
            pltpu.make_async_copy(
                stage.at[pl.ds(i * rows, rows), :],
                grad_o.at[pl.ds(pl.multiple_of(block_of(k) * BLOCK + start, rows), rows), :],
                sem.at[i])
            for i, k in enumerate(blocks)
        ]
        for c in copies:
            c.start()
        for c in copies:
            c.wait()


def out_proj(blocks, start, ds0, ds1, attn_out, w_out, prev, deps=(), tile=512):
    rows, width = ds0.shape
    tokens, cols = attn_out.shape
    per = BLOCK // rows
    o_specs = [pl.BlockSpec((rows, cols), functools.partial(lambda k, h: (block_of(k) * per + start // rows, 0), k),
                            pipeline_mode=pl.Buffered(1)) for k in blocks]
    w_spec = pl.BlockSpec((cols, tile), lambda h: (0, h))
    first = prev is None
    return pl.pallas_call(
        functools.partial(proj_body, blocks, start, first),
        grid=(width // tile,),
        in_specs=[pl.BlockSpec((rows, tile), lambda h: (0, h))] * 2 + o_specs + [w_spec]
        + ([] if first else [w_spec, ANY]) + [ANY] * len(deps),
        out_specs=[ANY, w_spec],
        out_shape=[jax.ShapeDtypeStruct((tokens, cols), BF16), jax.ShapeDtypeStruct((cols, width), F32)],
        scratch_shapes=[pltpu.VMEM((2 * rows, cols), F32), pltpu.VMEM((2 * rows, cols), BF16), pltpu.SemaphoreType.DMA((2,))],
        input_output_aliases={} if first else {5: 1, 6: 0},
        compiler_params=params(24 << 20),
        cost_estimate=pl.CostEstimate(flops=8 * rows * width * cols, bytes_accessed=8 << 20, transcendentals=0),
    )(*hbm(ds0, ds1, attn_out, attn_out, w_out, *([] if first else [prev[1], prev[0]]), *deps))


CHUNK = 256


def solution(mesh):
    token_spec = P(("dp", "tp"), None)
    split_cols = P("dp", "tp")
    weight_cols = P(None, "tp")
    weight_rows = P("tp", None)

    def cross(a):
        return lax.ppermute(a, "tp", CROSS)

    def pair(a):
        return lax.ppermute(a, "tp", PAIR)

    def after(a, *others):
        return lax.optimization_barrier((a,) + others)[0]

    def body(x_norm, grad_y, u_gate, u_up, w_gate, w_up, w_down, x_in, gamma, grad_res, attn_out, w_out):
        gamma = gamma.reshape(1, -1)
        gy_far = cross(grad_y)
        gy_sib = pair(grad_y)
        x_far = cross(x_norm)
        x_sib = pair(x_norm)
        starts = range(0, BLOCK, CHUNK)

        args = (u_gate, u_up, w_down, w_gate, w_up)
        dg_near, du_near, z_near, p_own, p_sib = hidden((OWN, SIB), (grad_y, gy_sib), 0, BLOCK, *args)
        p_pair = pair(p_sib)
        gy_far = after(gy_far, p_own)
        gy_diag = pair(gy_far)
        dgs, dus, zs, sends, deps = [], [], [], [], ()
        for at in starts:
            dg, du, z, p_far, p_diag = hidden((FAR, DIAG), (gy_far, gy_diag), at, CHUNK, *args, deps=deps)
            p_sum = add(p_far, pair(p_diag))
            dgs.append(dg), dus.append(du), zs.append(z), sends.append(p_sum)
            deps = (p_sum,)
        recvs = [cross(s) for s in sends]

        def pieces(own, sib, far, diag):
            return [(own, 0, BLOCK), (sib, 0, BLOCK)] + [(a, at, CHUNK) for at in starts for a in (far, diag)]

        def stacked(near, fars):
            return [(near, 0, BLOCK), (near, BLOCK, BLOCK)] + [(a, at, CHUNK) for a in fars for at in (0, CHUNK)]

        x_far = after(x_far, sends[-1])
        x_diag = pair(x_far)
        gw_down = weight_grad(stacked(z_near, zs), pieces(grad_y, gy_sib, gy_far, gy_diag), deps=(sends[-1],))
        xs = pieces(x_norm, x_sib, x_far, x_diag)

        whole, fars, prev = None, [], gw_down
        grads = []
        for c, at in enumerate(starts):
            piece, whole = norm_backward(at, p_own, p_pair, after(recvs[c], prev), x_in, grad_res, gamma, whole)
            fars.append(cross(piece))
            rights = stacked(*((dg_near, dgs), (du_near, dus))[c])
            prev = weight_grad(xs, rights, deps=(piece,))
            grads.append(prev)
        sib = pair(whole)
        res = out_proj((OWN, SIB), 0, whole, sib, attn_out, w_out, None, deps=(grads[1],))
        for c, at in enumerate(starts):
            far = after(fars[c], res[1])
            res = out_proj((FAR, DIAG), at, far, pair(far), attn_out, w_out, res)
        grad_attn, gw_out = res
        return whole, grad_attn, grads[0], grads[1], gw_down, gw_out


    return jax.shard_map(
        body,
        mesh=mesh,
        in_specs=(token_spec, token_spec, split_cols, split_cols, weight_cols, weight_cols, weight_rows,
                  token_spec, P(None), token_spec, split_cols, weight_rows),
        out_specs=(token_spec, split_cols, split_cols, split_cols, token_spec, token_spec),
        check_vma=False,
    )
```

time: 430 us -> 265 us (0.62); the launches traced: 421 us -> 265 us
  Pallas kernels: 0 us -> 198 us
  matrix products: 180 us -> 0 us
  waiting for transfers between devices: 178 us -> 46.1 us
  local copies, waits for them, and re-layouts: 40.5 us -> 9.77 us
  between operations: 14.2 us -> 0.97 us
  starting transfers between devices: 0.16 us -> 10.4 us
  other arithmetic: 8.98 us -> 0 us
    pallas_call x0 -> x13, Pallas kernels: none -> 198 us  [the longest x3 82.4 us: hidden(): pl.pallas_call(functools.partial(hidden_body, n, tiles), grid=(tiles + 1,...]
    dot_general x8 -> x0, matrix products: 180 us -> none  [the longest x1 31.5 us: local_backward(): lax.dot_general(gy_full, w_down, CONTRACT_COLS, preferred_element_type=jn...]
    all_gather x3 -> x0, waiting for transfers between devices: 110 us -> none  [the longest x1 61.1 us: local_backward(): gy_full = lax.all_gather(grad_y, 'tp', axis=0, tiled=True)]
    reduce_scatter x1 -> x0, waiting for transfers between devices: 66.2 us -> none  [local_backward(): lax.psum_scatter(part_x.astype(jnp.bfloat16), 'tp', scatter_dimension=0,...]
    ppermute x0 -> x16, waiting for transfers between devices: none -> 46.1 us  [the longest x6 32.2 us: cross(): return lax.ppermute(a, 'tp', CROSS)]
    unnamed x7 -> x32, local copies, waits for them, and re-layouts: 40.5 us -> 9.17 us
    ppermute x0 -> x16, starting transfers between devices: none -> 10.4 us  [the longest x6 8.54 us: cross(): return lax.ppermute(a, 'tp', CROSS)]
    convert_element_type x2 -> x0, other arithmetic: 5.7 us -> none  [the longest x1 5.69 us: rms_backward(): return (grad_res.astype(jnp.float32) + inv_rms * (scaled - xin_f * (inv_r...]
  transfers between devices with their start and end apart: 4 -> 16, of which waited for: 3 -> 9; matrix products, arithmetic and copies ran while one was open for 29% -> 0% of each run, Pallas kernels for 0% -> 61%
where the time goes in v1:
time: 265 us
  Pallas kernels  198 us (75%)
  waiting for transfers between devices  46.1 us (17%)
  starting transfers between devices  10.4 us (4%)
  local copies, waits for them, and re-layouts  9.77 us (4%)
    pallas_call x3, Pallas kernels, hidden(): pl.pallas_call(functools.partial(hidden_body, n, tiles), grid=(tiles + 1,...  82.4 us
    pallas_call x3, Pallas kernels, weight_grad(): pl.pallas_call(functools.partial(grad_body, n), grid=(cols // tn, m // tm...  73 us
    ppermute x6, waiting for transfers between devices, cross(): return lax.ppermute(a, 'tp', CROSS)  32.2 us
    pallas_call x3, Pallas kernels, out_proj(): pl.pallas_call(functools.partial(proj_body, blocks, start, first), grid=(...  27.1 us
    ppermute x10, waiting for transfers between devices, pair(): return lax.ppermute(a, 'tp', PAIR)  13.9 us
    pallas_call x2, Pallas kernels, norm_backward(): pl.pallas_call(norm_body, grid=(rows // tile,), in_specs=[here, here, par...  10.1 us
    unnamed x32, local copies, waits for them, and re-layouts  9.17 us
    ppermute x6, starting transfers between devices, cross(): return lax.ppermute(a, 'tp', CROSS)  8.54 us
  transfers between devices with their start and end apart: 16, of which 9 were waited for; matrix products, arithmetic and copies ran while one was open for 0% of the time, Pallas kernels for 61%

profile of v1, /device:TPU:0, one launch (start us, length us, event | category | flops | bytes accessed | tf_op | source)
XLA Modules:
  0.0 264.8 jit_solution(13927006950432904774)
XLA Ops:
  1.4 2.5 collective-permute-start.2
  3.9 1.6 collective-permute-done.refs_1_.refs_7_
  5.5 38.8 %shard_map.163 = (bf16[1024,2048]{1,0:T(8,128)(2,1)}, bf16[1024,2048]{1,0:T(8,128)(2,1)}, bf16[1024,2048]{1,0:T(8,128)(2,1)}, bf16[512,2048]{1,0:T(8,128)(2,1)}, bf16[512,2048]{1,0:T(8,128)(2,1)}) custom-call(bf16[512,2048]{1,0:T(8,128)(2,1)} %refs_6_.7, bf16[512,2048]{1,0:T(8,128)(2,1)} %collective-permute-done.refs_1_.refs_7_, bf16[2048,2048]{1,0:T(8,128)(2,1)} %refs_3_.8, ...), custom_call_target="tpu_custom_call" | custom-call | flops 25769803776 | bytes 52428800 | tf_op jit(solution)/shard_map/pallas_call | solution.py:101
  44.4 6.0 %collective-permute-done.2.refs_0_.refs_8_.refs_10_ = bf16[512,2048]{1,0:T(8,128)(2,1)S(1)} collective-permute-done((bf16[512,2048]{1,0:T(8,128)(2,1)}, bf16[512,2048]{1,0:T(8,128)(2,1)S(1)}, u32[]{:S(2)}, u32[]{:S(2)}) %collective-permute-start.2) | collective-permute-done | bytes 2097184 | tf_op jit(solution)/shard_map/ppermute | solution.py:251
  50.4 4.3 %collective-permute-done.3.refs_1_.refs_9_.refs_11_ = bf16[512,2048]{1,0:T(8,128)(2,1)} collective-permute-done((bf16[512,2048]{1,0:T(8,128)(2,1)S(1)}, bf16[512,2048]{1,0:T(8,128)(2,1)}, u32[]{:S(2)}, u32[]{:S(2)}) %collective-permute-start.3) | collective-permute-done | bytes 2097184 | tf_op jit(solution)/shard_map/ppermute | solution.py:254
  54.7 21.8 %shard_map.164 = (bf16[512,2048]{1,0:T(8,128)(2,1)}, bf16[512,2048]{1,0:T(8,128)(2,1)}, bf16[512,2048]{1,0:T(8,128)(2,1)}, bf16[256,2048]{1,0:T(8,128)(2,1)}, bf16[256,2048]{1,0:T(8,128)(2,1)}) custom-call(bf16[512,2048]{1,0:T(8,128)(2,1)} %copy-done.7, bf16[512,2048]{1,0:T(8,128)(2,1)} %collective-permute-done.3.refs_1_.refs_9_.refs_11_, ...), custom_call_target="tpu_custom_call" | custom-call | flops 12884901888 | bytes 52428800 | tf_op jit(solution)/shard_map/pallas_call | solution.py:101
  76.6 1.7 collective-permute-start.8
  78.4 1.0 collective-permute-done.4.b
  80.3 2.4 shard_map.165.refs_9_
  83.7 21.8 %shard_map.166 = (bf16[512,2048]{1,0:T(8,128)(2,1)}, bf16[512,2048]{1,0:T(8,128)(2,1)}, bf16[512,2048]{1,0:T(8,128)(2,1)}, bf16[256,2048]{1,0:T(8,128)(2,1)}, bf16[256,2048]{1,0:T(8,128)(2,1)}) custom-call(bf16[512,2048]{1,0:T(8,128)(2,1)} %copy-done.7, bf16[512,2048]{1,0:T(8,128)(2,1)} %collective-permute-done.3.refs_1_.refs_9_.refs_11_, ...), custom_call_target="tpu_custom_call" | custom-call | flops 12884901888 | bytes 52428800 | tf_op jit(solution)/shard_map/pallas_call | solution.py:101
  106.2 2.2 collective-permute-done.5.b
  108.5 1.0 copy-done.13
  109.5 2.4 shard_map.167.refs_12_
  111.9 13.0 %collective-permute-done.8.refs_2_.refs_4_ = bf16[512,2048]{1,0:T(8,128)(2,1)} collective-permute-done((bf16[512,2048]{1,0:T(8,128)(2,1)}, bf16[512,2048]{1,0:T(8,128)(2,1)}, u32[]{:S(2)}, u32[]{:S(2)}) %collective-permute-start.8) | collective-permute-done | bytes 2097184 | tf_op jit(solution)/shard_map/ppermute | solution.py:251
  125.5 1.7 collective-permute-start.10
  127.5 24.3 %shard_map.168 = f32[2048,2048]{1,0:T(8,128)} custom-call(bf16[1024,2048]{1,0:T(8,128)(2,1)} %get-tuple-element.48.refs_0_.refs_1_, bf16[1024,2048]{1,0:T(8,128)(2,1)} %get-tuple-element.48.refs_0_.refs_1_, bf16[512,2048]{1,0:T(8,128)(2,1)} %get-tuple-element.49.refs_2_.refs_3_, bf16[512,2048]{1,0:T(8,128)(2,1)} %get-tuple-element.49.refs_2_.refs_3_, ...), custom_call_target="tpu_custom_call" | custom-call | flops 17179869184 | bytes 33554432 | tf_op jit(solution)/shard_map/pallas_call | solution.py:128
  151.9 5.1 %shard_map.169 = (bf16[256,2048]{1,0:T(8,128)(2,1)S(1)}, bf16[512,2048]{1,0:T(8,128)(2,1)}) custom-call(bf16[512,2048]{1,0:T(8,128)(2,1)} %get-tuple-element.37.p_own, bf16[512,2048]{1,0:T(8,128)(2,1)} %collective-permute-done.1.p_pair, bf16[256,2048]{1,0:T(8,128)(2,1)} %collective-permute-done.10.p_far, bf16[512,2048]{1,0:T(8,128)(2,1)} %x_in.3, ...), custom_call_target="tpu_custom_call" | custom-call | flops 1048576000 | bytes 7340032 | tf_op jit(solution)/shard_map/pallas_call | solution.py:175
  156.9 1.0 copy-done.5
  157.9 24.3 %shard_map.170 = f32[2048,2048]{1,0:T(8,128)} custom-call(bf16[512,2048]{1,0:T(8,128)(2,1)} %refs_0_.5, bf16[512,2048]{1,0:T(8,128)(2,1)} %collective-permute-done.7.refs_1_, bf16[512,2048]{1,0:T(8,128)(2,1)} %collective-permute-done.8.refs_2_.refs_4_, bf16[512,2048]{1,0:T(8,128)(2,1)} %collective-permute-done.9.refs_3_.refs_5_, ...), custom_call_target="tpu_custom_call" | custom-call | flops 17179869184 | bytes 33554432 | tf_op jit(solution)/shard_map/pallas_call | solution.py:128
  183.2 5.1 %shard_map.171 = (bf16[256,2048]{1,0:T(8,128)(2,1)S(1)}, bf16[512,2048]{1,0:T(8,128)(2,1)}) custom-call(bf16[512,2048]{1,0:T(8,128)(2,1)} %get-tuple-element.37.p_own, bf16[512,2048]{1,0:T(8,128)(2,1)} %collective-permute-done.1.p_pair, bf16[256,2048]{1,0:T(8,128)(2,1)} %copy-done.12, bf16[512,2048]{1,0:T(8,128)(2,1)} %x_in.3, ...), custom_call_target="tpu_custom_call", output_to_operand_aliasing={{1}: (6, {})} | custom-call | flops 1048576000 | bytes 7340032 | tf_op jit(solution)/shard_map/pallas_call | solution.py:175
  188.3 1.0 copy-done.3
  189.3 1.7 collective-permute-start.12
  191.0 24.3 %shard_map.172.refs_5_ = f32[2048,2048]{1,0:T(8,128)} custom-call(bf16[512,2048]{1,0:T(8,128)(2,1)} %refs_0_.5, bf16[512,2048]{1,0:T(8,128)(2,1)} %collective-permute-done.7.refs_1_, bf16[512,2048]{1,0:T(8,128)(2,1)} %collective-permute-done.8.refs_2_.refs_4_, bf16[512,2048]{1,0:T(8,128)(2,1)} %collective-permute-done.9.refs_3_.refs_5_, ...), custom_call_target="tpu_custom_call" | custom-call | flops 17179869184 | bytes 33554432 | tf_op jit(solution)/shard_map/pallas_call | solution.py:128
  215.4 1.4 copy-done.8
  216.7 10.1 %shard_map.173 = (bf16[2048,512]{1,0:T(8,128)(2,1)}, f32[512,2048]{1,0:T(8,128)}) custom-call(bf16[512,2048]{1,0:T(8,128)(2,1)} %get-tuple-element.31.refs_0_, bf16[512,2048]{1,0:T(8,128)(2,1)} %copy-done.8, bf16[2048,512]{1,0:T(8,128)(2,1)} %refs_3_.11, bf16[2048,512]{1,0:T(8,128)(2,1)} %refs_3_.11, bf16[512,2048]{1,0:T(8,128)(2,1)} %refs_4_.11, ...), custom_call_target="tpu_custom_call" | custom-call | flops 4294967296 | bytes 8388608 | tf_op jit(solution)/shard_map/pallas_call | solution.py:227
  227.6 2.1 collective-permute-done.14.refs_1_
  229.8 1.0 copy-done.10
  230.7 8.5 %shard_map.174 = (bf16[2048,512]{1,0:T(8,128)(2,1)}, f32[512,2048]{1,0:T(8,128)}) custom-call(bf16[256,2048]{1,0:T(8,128)(2,1)} %collective-permute-done.12.refs_0_, bf16[256,2048]{1,0:T(8,128)(2,1)} %copy-done.10, bf16[2048,512]{1,0:T(8,128)(2,1)} %refs_3_.11, bf16[2048,512]{1,0:T(8,128)(2,1)} %refs_3_.11, ...), custom_call_target="tpu_custom_call", output_to_operand_aliasing={{1}: (5, {}), {0}: (6, {})} | custom-call | flops 2147483648 | bytes 8388608 | tf_op jit(solution)/shard_map/pallas_call | solution.py:227
  239.3 13.2 %collective-permute-done.11.refs_0_ = bf16[256,2048]{1,0:T(8,128)(2,1)S(1)} collective-permute-done((bf16[256,2048]{1,0:T(8,128)(2,1)S(1)}, bf16[256,2048]{1,0:T(8,128)(2,1)S(1)}, u32[]{:S(2)}, u32[]{:S(2)}) %collective-permute-start.11) | collective-permute-done | bytes 1048608 | tf_op jit(solution)/shard_map/ppermute | solution.py:251
  252.5 2.7 %collective-permute-done.15.refs_1_ = bf16[256,2048]{1,0:T(8,128)(2,1)S(1)} collective-permute-done((bf16[256,2048]{1,0:T(8,128)(2,1)S(1)}, bf16[256,2048]{1,0:T(8,128)(2,1)S(1)}, u32[]{:S(2)}, u32[]{:S(2)}) %collective-permute-start.15) | collective-permute-done | bytes 1048608 | tf_op jit(solution)/shard_map/ppermute | solution.py:254
  255.1 1.0 copy-done.11
  256.1 8.5 %shard_map.175 = (bf16[2048,512]{1,0:T(8,128)(2,1)}, f32[512,2048]{1,0:T(8,128)}) custom-call(bf16[256,2048]{1,0:T(8,128)(2,1)} %copy-done.9, bf16[256,2048]{1,0:T(8,128)(2,1)} %copy-done.11, bf16[2048,512]{1,0:T(8,128)(2,1)} %refs_3_.11, bf16[2048,512]{1,0:T(8,128)(2,1)} %refs_3_.11, ...), custom_call_target="tpu_custom_call", output_to_operand_aliasing={{1}: (5, {}), {0}: (6, {})} | custom-call | flops 2147483648 | bytes 8388608 | tf_op jit(solution)/shard_map/pallas_call | solution.py:227
  (46 shorter events, 6.2 us)
Async XLA Ops:
  0.6 4.9 %collective-permute-start = (bf16[512,2048]{1,0:T(8,128)(2,1)}, bf16[512,2048]{1,0:T(8,128)(2,1)}, u32[]{:S(2)}, u32[]{:S(2)}) collective-permute-start(bf16[512,2048]{1,0:T(8,128)(2,1)} %refs_6_.7), channel_id=1, source_target_pairs={{0,1},{1,0},{2,3},{3,2},{4,5},{5,4},{6,7},{7,6},{8,9},{9,8},{10,11... | collective-permute-start | bytes 6291464 | tf_op jit(solution)/shard_map/ppermute | solution.py:254
  1.4 49.0 %collective-permute-start.2 = (bf16[512,2048]{1,0:T(8,128)(2,1)}, bf16[512,2048]{1,0:T(8,128)(2,1)S(1)}, u32[]{:S(2)}, u32[]{:S(2)}) collective-permute-start(bf16[512,2048]{1,0:T(8,128)(2,1)} %refs_6_.7), channel_id=1, source_target_pairs={{0,2},{2,0},{1,3},{3,1},{4,6},{6,4},{5,7},{7,5},{8,10},{10,8},{9,1... | collective-permute-start | bytes 6291464 | tf_op jit(solution)/shard_map/ppermute | solution.py:251
  50.4 4.3 %copy-start.7 = (bf16[512,2048]{1,0:T(8,128)(2,1)}, bf16[512,2048]{1,0:T(8,128)(2,1)S(1)}, u32[]{:S(2)}) copy-start(bf16[512,2048]{1,0:T(8,128)(2,1)S(1)} %collective-permute-done.2.refs_0_.refs_8_.refs_10_) | copy-start | bytes 6291460
  50.4 4.3 %collective-permute-start.3 = (bf16[512,2048]{1,0:T(8,128)(2,1)S(1)}, bf16[512,2048]{1,0:T(8,128)(2,1)}, u32[]{:S(2)}, u32[]{:S(2)}) collective-permute-start(bf16[512,2048]{1,0:T(8,128)(2,1)S(1)} %collective-permute-done.2.refs_0_.refs_8_.refs_10_), channel_id=1, source_target_pairs={{0,1},{1,0},{2,3},{3,2},{4,5},{5,4},{6,7},{7,6},{8,9},{9,8},{10,11... | collective-permute-start | bytes 6291464 | tf_op jit(solution)/shard_map/ppermute | solution.py:254
  76.5 2.9 %collective-permute-start.4 = (bf16[256,2048]{1,0:T(8,128)(2,1)}, bf16[256,2048]{1,0:T(8,128)(2,1)S(1)}, u32[]{:S(2)}, u32[]{:S(2)}) collective-permute-start(bf16[256,2048]{1,0:T(8,128)(2,1)} %get-tuple-element.41), channel_id=1, source_target_pairs={{0,1},{1,0},{2,3},{3,2},{4,5},{5,4},{6,7},{7,6},{8,9},{9,8},{10,11... | collective-permute-start | bytes 3145736 | tf_op jit(solution)/shard_map/ppermute | solution.py:254
  76.6 48.2 %collective-permute-start.8 = (bf16[512,2048]{1,0:T(8,128)(2,1)}, bf16[512,2048]{1,0:T(8,128)(2,1)}, u32[]{:S(2)}, u32[]{:S(2)}) collective-permute-start(bf16[512,2048]{1,0:T(8,128)(2,1)} %refs_0_.5), channel_id=1, source_target_pairs={{0,2},{2,0},{1,3},{3,1},{4,6},{6,4},{5,7},{7,5},{8,10},{10,8},{9,1... | collective-permute-start | bytes 6291464 | tf_op jit(solution)/shard_map/ppermute | solution.py:251
  79.4 1.0 copy-start.14
  82.7 1.0 copy-start
  105.5 19.3 %copy-start.15 = (bf16[2048]{0:T(1024)(128)(2,1)S(1)}, bf16[2048]{0:T(1024)(128)(2,1)}, u32[]{:S(2)}) copy-start(bf16[2048]{0:T(1024)(128)(2,1)} %param.20) | copy-start | bytes 12292
  105.5 19.9 %copy-start.1 = (bf16[256,2048]{1,0:T(8,128)(2,1)S(1)}, bf16[256,2048]{1,0:T(8,128)(2,1)}, u32[]{:S(2)}) copy-start(bf16[256,2048]{1,0:T(8,128)(2,1)} %copy-done) | copy-start | bytes 3145732
  105.5 2.9 %collective-permute-start.5 = (bf16[256,2048]{1,0:T(8,128)(2,1)}, bf16[256,2048]{1,0:T(8,128)(2,1)S(1)}, u32[]{:S(2)}, u32[]{:S(2)}) collective-permute-start(bf16[256,2048]{1,0:T(8,128)(2,1)} %get-tuple-element.43), channel_id=1, source_target_pairs={{0,1},{1,0},{2,3},{3,2},{4,5},{5,4},{6,7},{7,6},{8,9},{9,8},{10,11... | collective-permute-start | bytes 3145736 | tf_op jit(solution)/shard_map/ppermute | solution.py:254
  105.7 46.1 %collective-permute-start.1 = (bf16[512,2048]{1,0:T(8,128)(2,1)}, bf16[512,2048]{1,0:T(8,128)(2,1)}, u32[]{:S(2)}, u32[]{:S(2)}) collective-permute-start(bf16[512,2048]{1,0:T(8,128)(2,1)} %get-tuple-element.38), channel_id=1, source_target_pairs={{0,1},{1,0},{2,3},{3,2},{4,5},{5,4},{6,7},{7,6},{8,9},{9,8},{10,11... | collective-permute-start | bytes 6291464 | tf_op jit(solution)/shard_map/ppermute | solution.py:254
  106.1 51.8 %collective-permute-start.7 = (bf16[512,2048]{1,0:T(8,128)(2,1)}, bf16[512,2048]{1,0:T(8,128)(2,1)}, u32[]{:S(2)}, u32[]{:S(2)}) collective-permute-start(bf16[512,2048]{1,0:T(8,128)(2,1)} %refs_0_.5), channel_id=1, source_target_pairs={{0,1},{1,0},{2,3},{3,2},{4,5},{5,4},{6,7},{7,6},{8,9},{9,8},{10,11... | collective-permute-start | bytes 6291464 | tf_op jit(solution)/shard_map/ppermute | solution.py:254
  108.5 1.0 copy-start.13
  111.9 15.6 %copy-start.2 = (bf16[256,2048]{1,0:T(8,128)(2,1)}, bf16[256,2048]{1,0:T(8,128)(2,1)S(1)}, u32[]{:S(2)}) copy-start(bf16[256,2048]{1,0:T(8,128)(2,1)S(1)} %shard_map.167.refs_12_) | copy-start | bytes 3145732
  124.9 33.0 %collective-permute-start.9 = (bf16[512,2048]{1,0:T(8,128)(2,1)}, bf16[512,2048]{1,0:T(8,128)(2,1)}, u32[]{:S(2)}, u32[]{:S(2)}) collective-permute-start(bf16[512,2048]{1,0:T(8,128)(2,1)} %collective-permute-done.8.refs_2_.refs_4_), channel_id=1, source_target_pairs={{0,1},{1,0},{2,3},{3,2},{4,5},{5,4},{6,7},{7,6},{8,9},{9,8},{10,11... | collective-permute-start | bytes 6291464 | tf_op jit(solution)/shard_map/ppermute | solution.py:254
  125.5 26.4 %collective-permute-start.10 = (bf16[256,2048]{1,0:T(8,128)(2,1)S(1)}, bf16[256,2048]{1,0:T(8,128)(2,1)}, u32[]{:S(2)}, u32[]{:S(2)}) collective-permute-start(bf16[256,2048]{1,0:T(8,128)(2,1)S(1)} %copy-done.1), channel_id=1, source_target_pairs={{0,2},{2,0},{1,3},{3,1},{4,6},{6,4},{5,7},{7,5},{8,10},{10,8},{9,1... | collective-permute-start | bytes 3145736 | tf_op jit(solution)/shard_map/ppermute | solution.py:251
  127.2 55.0 %collective-permute-start.6 = (bf16[256,2048]{1,0:T(8,128)(2,1)S(1)}, bf16[256,2048]{1,0:T(8,128)(2,1)S(1)}, u32[]{:S(2)}, u32[]{:S(2)}) collective-permute-start(bf16[256,2048]{1,0:T(8,128)(2,1)S(1)} %shard_map.167.refs_12_), channel_id=1, source_target_pairs={{0,2},{2,0},{1,3},{3,1},{4,6},{6,4},{5,7},{7,5},{8,10},{10,8},{9,1... | collective-permute-start | bytes 3145736 | tf_op jit(solution)/shard_map/ppermute | solution.py:251
  156.9 1.0 copy-start.5
  182.2 1.0 copy-start.12
  183.2 6.0 %copy-start.6 = (bf16[256,2048]{1,0:T(8,128)(2,1)S(1)}, bf16[256,2048]{1,0:T(8,128)(2,1)}, u32[]{:S(2)}) copy-start(bf16[256,2048]{1,0:T(8,128)(2,1)} %copy-done.5) | copy-start | bytes 3145732
  188.3 1.0 copy-start.3
  189.3 26.1 %collective-permute-start.13 = (bf16[512,2048]{1,0:T(8,128)(2,1)}, bf16[512,2048]{1,0:T(8,128)(2,1)S(1)}, u32[]{:S(2)}, u32[]{:S(2)}) collective-permute-start(bf16[512,2048]{1,0:T(8,128)(2,1)} %get-tuple-element.31.refs_0_), channel_id=1, source_target_pairs={{0,1},{1,0},{2,3},{3,2},{4,5},{5,4},{6,7},{7,6},{8,9},{9,8},{10,11... | collective-permute-start | bytes 6291464 | tf_op jit(solution)/shard_map/ppermute | solution.py:254
  189.3 37.6 %collective-permute-start.12 = (bf16[256,2048]{1,0:T(8,128)(2,1)S(1)}, bf16[256,2048]{1,0:T(8,128)(2,1)}, u32[]{:S(2)}, u32[]{:S(2)}) collective-permute-start(bf16[256,2048]{1,0:T(8,128)(2,1)S(1)} %copy-done.6), channel_id=1, source_target_pairs={{0,2},{2,0},{1,3},{3,1},{4,6},{6,4},{5,7},{7,5},{8,10},{10,8},{9,1... | collective-permute-start | bytes 3145736 | tf_op jit(solution)/shard_map/ppermute | solution.py:251
  215.3 11.8 %copy-start.4 = (bf16[256,2048]{1,0:T(8,128)(2,1)S(1)}, bf16[256,2048]{1,0:T(8,128)(2,1)}, u32[]{:S(2)}) copy-start(bf16[256,2048]{1,0:T(8,128)(2,1)} %copy-done.3) | copy-start | bytes 3145732
  215.4 1.4 copy-start.8
  226.9 2.9 %collective-permute-start.14 = (bf16[256,2048]{1,0:T(8,128)(2,1)}, bf16[256,2048]{1,0:T(8,128)(2,1)S(1)}, u32[]{:S(2)}, u32[]{:S(2)}) collective-permute-start(bf16[256,2048]{1,0:T(8,128)(2,1)} %collective-permute-done.12.refs_0_), channel_id=1, source_target_pairs={{0,1},{1,0},{2,3},{3,2},{4,5},{5,4},{6,7},{7,6},{8,9},{9,8},{10,11... | collective-permute-start | bytes 3145736 | tf_op jit(solution)/shard_map/ppermute | solution.py:254
  227.1 25.4 %collective-permute-start.11 = (bf16[256,2048]{1,0:T(8,128)(2,1)S(1)}, bf16[256,2048]{1,0:T(8,128)(2,1)S(1)}, u32[]{:S(2)}, u32[]{:S(2)}) collective-permute-start(bf16[256,2048]{1,0:T(8,128)(2,1)S(1)} %copy-done.4), channel_id=1, source_target_pairs={{0,2},{2,0},{1,3},{3,1},{4,6},{6,4},{5,7},{7,5},{8,10},{10,8},{9,1... | collective-permute-start | bytes 3145736 | tf_op jit(solution)/shard_map/ppermute | solution.py:251
  229.8 1.0 copy-start.10
  252.5 2.7 %copy-start.9 = (bf16[256,2048]{1,0:T(8,128)(2,1)}, bf16[256,2048]{1,0:T(8,128)(2,1)S(1)}, u32[]{:S(2)}) copy-start(bf16[256,2048]{1,0:T(8,128)(2,1)S(1)} %collective-permute-done.11.refs_0_) | copy-start | bytes 3145732
  252.5 2.7 %collective-permute-start.15 = (bf16[256,2048]{1,0:T(8,128)(2,1)S(1)}, bf16[256,2048]{1,0:T(8,128)(2,1)S(1)}, u32[]{:S(2)}, u32[]{:S(2)}) collective-permute-start(bf16[256,2048]{1,0:T(8,128)(2,1)S(1)} %collective-permute-done.11.refs_0_), channel_id=1, source_target_pairs={{0,1},{1,0},{2,3},{3,2},{4,5},{5,4},{6,7},{7,6},{8,9},{9,8},{10,11... | collective-permute-start | bytes 3145736 | tf_op jit(solution)/shard_map/ppermute | solution.py:254
  255.1 1.0 copy-start.11

commit v2 on v1

v2 whole, which is shorter than its diff:
```python
import functools

import jax
import jax.numpy as jnp
from jax import lax
from jax.experimental import pallas as pl
from jax.experimental.pallas import tpu as pltpu
from jax.sharding import PartitionSpec as P


F32 = jnp.float32
BF16 = jnp.bfloat16
NORM_EPS = 1e-5
ROWS_T = (((0,), (0,)), ((), ()))
COLS_T = (((1,), (1,)), ((), ()))
ANY = pl.BlockSpec(memory_space=pl.ANY)
VMEM_LIMIT = 60 * 1024 * 1024
ALL_VMEM = 67043328
BLOCK = 512

CROSS = [(0, 2), (2, 0), (1, 3), (3, 1)]
PAIR = [(0, 1), (1, 0), (2, 3), (3, 2)]
OWN, SIB, FAR, DIAG = 0, 1, 2, 3


def dot(a, b, dims):
    return lax.dot_general(a, b, dims, preferred_element_type=F32)


def block_of(k):
    return lax.axis_index("tp") ^ k


def params(limit=VMEM_LIMIT):
    return pltpu.CompilerParams(vmem_limit_bytes=limit)


def hbm(*arrays):
    return [pltpu.with_memory_space_constraint(a, pltpu.HBM) for a in arrays]


def once(shape, index=None):
    return pl.BlockSpec(shape, index or (lambda *_: (0,) * len(shape)), pipeline_mode=pl.Buffered(1))


def hidden_body(n, tiles, parts, down, *refs):
    dys, ugs, uus = refs[:n], refs[n:2 * n], refs[2 * n:3 * n]
    wd, wg, wu = refs[3 * n:3 * n + 3]
    m = n * parts
    outs = refs[-(m + 5 + (down > 0) + (down < n)):-(m + 3)]
    dg, du = outs[:2]
    ps, (acc, held_g, held_u) = refs[-(m + 3):-3], refs[-3:]
    step = pl.program_id(0)
    rows = dys[0].shape[0]
    piece = rows // parts

    def form(slot):
        total = None
        for i in range(n):
            span = pl.ds(i * rows, rows)
            grad_h = dot(dys[i][...], wd[...], COLS_T)
            gate = ugs[i][...].astype(F32)
            up = uus[i][...].astype(F32)
            sig = jax.nn.sigmoid(gate)
            act = gate * sig
            hidden_z = (act * up).astype(BF16)
            grad_up = (grad_h * act).astype(BF16)
            grad_gate = (grad_h * up * (sig * (1.0 + gate * (1.0 - sig)))).astype(BF16)
            du[span, :] = grad_up
            dg[span, :] = grad_gate
            held_u[slot, span, :] = grad_up
            held_g[slot, span, :] = grad_gate
            if i < down:
                more = dot(hidden_z, dys[i][...], ROWS_T)
                total = more if total is None else total + more
            else:
                outs[-1][pl.ds((i - down) * rows, rows), :] = hidden_z
        if down:
            outs[2][...] = total

    def term(slot):
        return dot(held_g[slot], wg[...], COLS_T) + dot(held_u[slot], wu[...], COLS_T)

    @pl.when(step == 0)
    def _():
        form(0)

    @pl.when((step > 0) & (step < tiles))
    def _():
        slot = lax.rem(step, 2)
        acc[...] = jnp.where(step == 1, 0.0, acc[...]) + term(1 - slot)
        form(slot)

    @pl.when(step == tiles)
    def _():
        total = acc[...] + term((tiles - 1) % 2)
        for i in range(m):
            ps[i][...] = total[i * piece:(i + 1) * piece].astype(BF16)


def hidden(blocks, dys, parts, down, u_gate, u_up, w_down, w_gate, w_up, deps=(), tile=512):
    n = len(blocks)
    rows, width = dys[0].shape
    cols = w_down.shape[0]
    tiles = cols // tile
    now = lambda s: jnp.minimum(s, tiles - 1)
    before = lambda s: jnp.maximum(s - 1, 0)
    u_specs = [pl.BlockSpec((rows, tile), functools.partial(lambda k, s: (block_of(k), now(s)), k)) for k in blocks]
    tile_out = pl.BlockSpec((n * rows, tile), lambda s: (0, now(s)))
    z_out = pl.BlockSpec(((n - down) * rows, tile), lambda s: (0, now(s)))
    w_late = pl.BlockSpec((width, tile), lambda s: (0, before(s)))
    w_now = pl.BlockSpec((tile, width), lambda s: (now(s), 0))
    wide = jax.ShapeDtypeStruct((n * rows, cols), BF16)
    piece = (rows // parts, width)
    return pl.pallas_call(
        functools.partial(hidden_body, n, tiles, parts, down),
        grid=(tiles + 1,),
        in_specs=[once((rows, width))] * n + u_specs + u_specs + [w_now, w_late, w_late] + [ANY] * len(deps),
        out_specs=[tile_out] * 2 + [w_now] * (down > 0) + [z_out] * (down < n) + [once(piece)] * (n * parts),
        out_shape=[wide] * 2 + [jax.ShapeDtypeStruct((cols, width), F32)] * (down > 0)
        + [jax.ShapeDtypeStruct(((n - down) * rows, cols), BF16)] * (down < n)
        + [jax.ShapeDtypeStruct(piece, BF16)] * (n * parts),
        scratch_shapes=[pltpu.VMEM((n * rows, width), F32)] + [pltpu.VMEM((2, n * rows, tile), BF16)] * 2,
        compiler_params=params(),
        cost_estimate=pl.CostEstimate(flops=(6 * n + 2 * down) * rows * width * cols, bytes_accessed=50 << 20,
                                      transcendentals=n * rows * cols),
    )(*dys, *hbm(*([u_gate] * n), *([u_up] * n), w_down, w_gate, w_up, *deps))


def grad_body(n, *refs):
    lefts, rights, out = refs[:n], refs[n:2 * n], refs[-1]
    total = dot(lefts[0][...], rights[0][...], ROWS_T)
    for a, b in zip(lefts[1:], rights[1:]):
        total += dot(a[...], b[...], ROWS_T)
    out[...] = total


def grad_more_body(n, *refs):
    lefts, rights, prev, out = refs[:n], refs[n:2 * n], refs[2 * n], refs[-1]
    total = prev[...]
    for a, b in zip(lefts, rights):
        total += dot(a[...], b[...], ROWS_T)
    out[...] = total


def weight_grad(lefts, rights, prev=None, deps=(), tm=256):
    n = len(lefts)
    m, cols = lefts[0][0].shape[1], rights[0][0].shape[1]
    l_specs = [pl.BlockSpec((BLOCK, tm), functools.partial(lambda b, i: (b, i), b)) for _, b in lefts]
    r_specs = [once((BLOCK, cols), functools.partial(lambda b, i: (b, 0), b)) for _, b in rights]
    out_spec = pl.BlockSpec((tm, cols), lambda i: (i, 0))
    more = [] if prev is None else [prev]
    return pl.pallas_call(
        functools.partial(grad_body if prev is None else grad_more_body, n),
        grid=(m // tm,),
        in_specs=l_specs + r_specs + [out_spec] * len(more) + [ANY] * len(deps),
        out_specs=out_spec,
        out_shape=jax.ShapeDtypeStruct((m, cols), F32),
        input_output_aliases={2 * n: 0} if more else {},
        compiler_params=params(),
        cost_estimate=pl.CostEstimate(flops=2 * n * BLOCK * m * cols, bytes_accessed=32 << 20, transcendentals=0),
    )(*hbm(*[a for a, _ in lefts], *[a for a, _ in rights], *more, *deps))


def spacer_body(*refs):
    refs[-1][...] = jnp.zeros_like(refs[-1])


def spacer(*deps):
    return pl.pallas_call(
        spacer_body,
        in_specs=[ANY] * len(deps),
        out_shape=jax.ShapeDtypeStruct((8, 128), F32),
        compiler_params=params(ALL_VMEM),
        cost_estimate=pl.CostEstimate(flops=1000, bytes_accessed=4096, transcendentals=0),
    )(*hbm(*deps))


def add_body(a, b, *refs):
    refs[-1][...] = (a[...].astype(F32) + b[...].astype(F32)).astype(BF16)


def add(a, b, tile=128):
    rows, width = a.shape
    spec = pl.BlockSpec((tile, width), lambda i: (i, 0))
    return pl.pallas_call(
        add_body,
        grid=(rows // tile,),
        in_specs=[spec, spec],
        out_specs=spec,
        out_shape=jax.ShapeDtypeStruct((rows, width), BF16),
        compiler_params=params(24 << 20),
        cost_estimate=pl.CostEstimate(flops=1000 * rows * width, bytes_accessed=6 * rows * width, transcendentals=0),
    )(*hbm(a), b)


def norm_body(p_own, p_pair, p_far, x_in, grad_res, gamma, *refs):
    piece, whole = refs[-2:]
    grad_x = (p_own[...].astype(F32) + p_pair[...].astype(F32) + p_far[...].astype(F32)).astype(BF16)
    xin = x_in[...].astype(F32)
    inv = lax.rsqrt(jnp.mean(xin * xin, axis=-1, keepdims=True) + NORM_EPS)
    scaled = grad_x.astype(F32) * gamma[...].astype(F32)
    proj = jnp.mean(scaled * xin, axis=-1, keepdims=True)
    res = (grad_res[...].astype(F32) + inv * (scaled - xin * (inv * inv) * proj)).astype(BF16)
    piece[...] = res
    whole[...] = res


def norm_backward(start, rows, p_own, p_pair, p_far, far_start, x_in, grad_res, gamma, prev, deps=(), tile=128):
    width = p_far.shape[1]
    first, far_first = start // tile, far_start // tile
    here = pl.BlockSpec((tile, width), lambda i: (first + i, 0))
    recv = pl.BlockSpec((tile, width), lambda i: (far_first + i, 0))
    part = pl.BlockSpec((tile, width), lambda i: (i, 0))
    extra = ([] if prev is None else [prev]) + list(deps)
    return pl.pallas_call(
        norm_body,
        grid=(rows // tile,),
        in_specs=[here, here, recv, here, here, once((1, width))] + [ANY] * len(extra),
        out_specs=[part, here],
        out_shape=[jax.ShapeDtypeStruct((rows, width), BF16), jax.ShapeDtypeStruct(p_own.shape, BF16)],
        input_output_aliases={} if prev is None else {6: 1},
        compiler_params=params(24 << 20),
        cost_estimate=pl.CostEstimate(flops=2000 * rows * width, bytes_accessed=14 * rows * width, transcendentals=0),
    )(*hbm(p_own, p_pair), p_far, *hbm(x_in, grad_res, gamma, *extra))


def proj_body(places, first, *refs):
    n = len(places)
    ds, o, w_out = refs[:n], refs[n:2 * n], refs[2 * n]
    grad_o, grad_w, acc, stage, sem = refs[-5:]
    step = pl.program_id(0)
    spans, at = [], 0
    for r in ds:
        spans.append(pl.ds(at, r.shape[0]))
        at += r.shape[0]

    @pl.when(step == 0)
    def _():
        acc[...] = jnp.zeros_like(acc)

    total = dot(o[0][...], ds[0][...], ROWS_T)
    for i in range(n):
        acc[spans[i], :] += dot(ds[i][...], w_out[...], COLS_T)
        if i:
            total += dot(o[i][...], ds[i][...], ROWS_T)
    grad_w[...] = total if first else refs[2 * n + 1][...] + total

    @pl.when(step == pl.num_programs(0) - 1)
    def _():
        stage[...] = acc[...].astype(BF16)
        copies = []
        for i, (k, start) in enumerate(places):
            rows = ds[i].shape[0]
            to = pl.ds(pl.multiple_of(block_of(k) * BLOCK + start, rows), rows)
            copies.append(pltpu.make_async_copy(stage.at[spans[i], :], grad_o.at[to, :], sem.at[i]))
        for c in copies:
            c.start()
        for c in copies:
            c.wait()


def out_proj(pieces, attn_out, w_out, prev, deps=(), tile=512):
    n = len(pieces)
    tokens, cols = attn_out.shape
    width = w_out.shape[1]
    sizes = [a.shape[0] for a, _, _ in pieces]
    places = [(k, start) for _, k, start in pieces]
    o_specs = [once((r, cols), functools.partial(lambda k, r, start, h: ((block_of(k) * BLOCK + start) // r, 0), k, r, start))
               for r, (k, start) in zip(sizes, places)]
    w_spec = pl.BlockSpec((cols, tile), lambda h: (0, h))
    first = prev is None
    return pl.pallas_call(
        functools.partial(proj_body, places, first),
        grid=(width // tile,),
        in_specs=[pl.BlockSpec((r, tile), lambda h: (0, h)) for r in sizes] + o_specs + [w_spec]
        + ([] if first else [w_spec, ANY]) + [ANY] * len(deps),
        out_specs=[ANY, w_spec],
        out_shape=[jax.ShapeDtypeStruct((tokens, cols), BF16), jax.ShapeDtypeStruct((cols, width), F32)],
        scratch_shapes=[pltpu.VMEM((sum(sizes), cols), F32), pltpu.VMEM((sum(sizes), cols), BF16), pltpu.SemaphoreType.DMA((n,))],
        input_output_aliases={} if first else {2 * n + 1: 1, 2 * n + 2: 0},
        compiler_params=params(24 << 20),
        cost_estimate=pl.CostEstimate(flops=4 * sum(sizes) * width * cols, bytes_accessed=8 << 20, transcendentals=0),
    )(*[a for a, _, _ in pieces], *hbm(*[attn_out] * n, w_out, *([] if first else [prev[1], prev[0]]), *deps))


def last_body(places, tile, *refs):
    n = len(places)
    ds, (o, w_out, prev_w) = refs[:n], refs[n:n + 3]
    grad_o, grad_w, held, stage, sem_w, sem_o = refs[-6:]
    rows = ds[0].shape[0]
    tiles = w_out.shape[1] // tile
    o_rows = [pl.ds(pl.multiple_of(block_of(k) * BLOCK + start, rows), rows) for k, start in places]

    def w_copy(h):
        cols = pl.ds(pl.multiple_of(h * tile, tile), tile)
        return pltpu.make_async_copy(held.at[:, cols], grad_w.at[:, cols], sem_w.at[h])

    def o_copy(i):
        return pltpu.make_async_copy(stage.at[pl.ds(i * rows, rows), :], grad_o.at[o_rows[i], :], sem_o.at[i])

    @pl.loop(0, tiles)
    def _(h):
        cols = pl.ds(pl.multiple_of(h * tile, tile), tile)
        total = dot(o[o_rows[0], :], ds[0][:, cols], ROWS_T)
        for i in range(1, n):
            total += dot(o[o_rows[i], :], ds[i][:, cols], ROWS_T)
        held[:, cols] = total + prev_w[:, cols]
        w_copy(h).start()

    for i in range(n):
        stage[pl.ds(i * rows, rows), :] = dot(ds[i][...], w_out[...], COLS_T).astype(BF16)
        o_copy(i).start()
    for i in range(n):
        o_copy(i).wait()
    for h in range(tiles):
        w_copy(h).wait()


def last_proj(pieces, attn_out, w_out, prev, tile=512):
    n = len(pieces)
    tokens, cols = attn_out.shape
    width = w_out.shape[1]
    rows = pieces[0][0].shape[0]
    return pl.pallas_call(
        functools.partial(last_body, [(k, start) for _, k, start in pieces], tile),
        in_specs=[pl.BlockSpec(memory_space=pltpu.VMEM)] * (n + 3) + [ANY],
        out_specs=[ANY, ANY],
        out_shape=[jax.ShapeDtypeStruct((tokens, cols), BF16), jax.ShapeDtypeStruct((cols, width), F32)],
        scratch_shapes=[pltpu.VMEM((cols, width), F32), pltpu.VMEM((n * rows, cols), BF16),
                        pltpu.SemaphoreType.DMA((width // tile,)), pltpu.SemaphoreType.DMA((n,))],
        input_output_aliases={n + 3: 0},
        compiler_params=params(16 << 20),
        cost_estimate=pl.CostEstimate(flops=4 * n * rows * width * cols, bytes_accessed=8 << 20, transcendentals=0),
    )(*[a for a, _, _ in pieces], attn_out, w_out, prev[1], *hbm(prev[0]))


DX_PARTS = 2
DS_PIECES = (256, 256)


def solution(mesh):
    token_spec = P(("dp", "tp"), None)
    split_cols = P("dp", "tp")
    weight_cols = P(None, "tp")
    weight_rows = P("tp", None)

    def cross(a):
        return lax.ppermute(a, "tp", CROSS)

    def pair(a):
        return lax.ppermute(a, "tp", PAIR)

    def after(a, *others):
        return lax.optimization_barrier((a,) + others)[0]

    def body(x_norm, grad_y, u_gate, u_up, w_gate, w_up, w_down, x_in, gamma, grad_res, attn_out, w_out):
        gamma = gamma.reshape(1, -1)
        gy_far = cross(grad_y)
        gy_sib = pair(grad_y)
        x_far = cross(x_norm)
        x_sib = pair(x_norm)
        gap = spacer(gamma)

        args = (u_gate, u_up, w_down, w_gate, w_up)
        dg_near, du_near, gw_down, z_sib, p_own, p_sib = hidden(
            (OWN, SIB), (grad_y, gy_sib), 1, 1, *args, deps=(gap,), tile=256)
        p_pair = pair(p_sib)
        gy_far = after(gy_far, p_own)
        gy_diag = pair(gy_far)
        gap = spacer(p_own)
        dg_far, du_far, z_far, *parts = hidden((FAR, DIAG), (gy_far, gy_diag), DX_PARTS, 0, *args, deps=(gap,))
        p_far, p_diag = parts[:DX_PARTS], parts[DX_PARTS:]
        p_diag = [pair(p) for p in p_diag]
        sends = [add(a, b) for a, b in zip(p_far, p_diag)]
        recvs = [cross(p) for p in sends]
        x_far = after(x_far, sends[-1])
        x_diag = pair(x_far)
        gw_down = weight_grad([(z_sib, 0), (z_far, 0), (z_far, 1)], [(gy_sib, 0), (gy_far, 0), (gy_diag, 0)],
                              prev=gw_down, deps=(sends[-1],), tm=512)

        xs = [(x_norm, 0), (x_sib, 0), (x_far, 0), (x_diag, 0)]
        rest = [functools.partial(weight_grad, xs, [(dg_near, 0), (dg_near, 1), (dg_far, 0), (dg_far, 1)]),
                functools.partial(weight_grad, xs, [(du_near, 0), (du_near, 1), (du_far, 0), (du_far, 1)])]
        dx_rows = BLOCK // DX_PARTS
        whole, fars, places, grads, at, prev = None, [], [], [], 0, gw_down
        for c, n in enumerate(DS_PIECES):
            part = at // dx_rows
            piece, whole = norm_backward(at, n, p_own, p_pair, after(recvs[part], prev), at - part * dx_rows,
                                         x_in, grad_res, gamma, whole)
            fars.append(cross(piece))
            places.append(at)
            prev = piece
            if c < len(rest):
                prev = rest[c](deps=(piece,))
                grads.append(prev)
            at += n
        gw_gate, gw_up = grads
        sib = pair(whole)
        near = out_proj([(whole, OWN, 0), (sib, SIB, 0)], attn_out, w_out, None, deps=(gw_up,), tile=2048)
        pieces, prev = [], gw_up
        for c, at in enumerate(places):
            far = after(fars[c], prev)
            pieces += [(far, FAR, at), (pair(far), DIAG, at)]
            prev = near[1]
        grad_attn, gw_out = last_proj(pieces, attn_out, w_out, near)
        return whole, grad_attn, gw_gate, gw_up, gw_down, gw_out


    return jax.shard_map(
        body,
        mesh=mesh,
        in_specs=(token_spec, token_spec, split_cols, split_cols, weight_cols, weight_cols, weight_rows,
                  token_spec, P(None), token_spec, split_cols, weight_rows),
        out_specs=(token_spec, split_cols, split_cols, split_cols, token_spec, token_spec),
        check_vma=False,
    )
```

time: 265 us -> 241 us (0.909)
  Pallas kernels: 198 us -> 179 us
  local copies, waits for them, and re-layouts: 9.77 us -> 1.3 us
  waiting for transfers between devices: 46.1 us -> 49.4 us
    pallas_call x11, Pallas kernels: 193 us -> 176 us  [the longest x2 81 us: hidden(): pl.pallas_call(functools.partial(hidden_body, n, tiles, parts, down), gri...]
    ppermute x6, waiting for transfers between devices: 32.2 us -> 42.5 us  [cross(): return lax.ppermute(a, 'tp', CROSS)]
    unnamed x32 -> x8, local copies, waits for them, and re-layouts: 9.17 us -> 0.02 us
    ppermute x10, waiting for transfers between devices: 13.9 us -> 6.9 us  [pair(): return lax.ppermute(a, 'tp', PAIR)]
  transfers between devices with their start and end apart: 16 -> 16, of which waited for: 9 -> 7; matrix products, arithmetic and copies ran while one was open for 0% -> 1% of each run, Pallas kernels for 61% -> 69%
where the time goes in v2:
time: 241 us
  Pallas kernels  179 us (74%)
  waiting for transfers between devices  49.4 us (20%)
  starting transfers between devices  10.2 us (4%)
    pallas_call x2, Pallas kernels, hidden(): pl.pallas_call(functools.partial(hidden_body, n, tiles, parts, down), gri...  81 us
    pallas_call x3, Pallas kernels, weight_grad(): pl.pallas_call(functools.partial(grad_body if prev is None else grad_more...  70.2 us
    ppermute x6, waiting for transfers between devices, cross(): return lax.ppermute(a, 'tp', CROSS)  42.5 us
    pallas_call x2, Pallas kernels, norm_backward(): pl.pallas_call(norm_body, grid=(rows // tile,), in_specs=[here, here, rec...  9.32 us
    ppermute x6, starting transfers between devices, cross(): return lax.ppermute(a, 'tp', CROSS)  8.36 us
    pallas_call x1, Pallas kernels, last_proj(): pl.pallas_call(functools.partial(last_body, [(k, start) for _, k, start i...  7.32 us
    pallas_call x1, Pallas kernels, out_proj(): pl.pallas_call(functools.partial(proj_body, places, first), grid=(width /...  7.17 us
    ppermute x10, waiting for transfers between devices, pair(): return lax.ppermute(a, 'tp', PAIR)  6.9 us
  transfers between devices with their start and end apart: 16, of which 7 were waited for; matrix products, arithmetic and copies ran while one was open for 1% of the time, Pallas kernels for 69%

profile of v2, /device:TPU:0, one launch (start us, length us, event | category | flops | bytes accessed | tf_op | source)
XLA Modules:
  0.0 240.7 jit_solution(2798727662837257652)
XLA Ops:
  0.6 0.8 collective-permute-start
  1.4 1.3 reshape.15.refs_0_.gamma
  2.7 2.5 %collective-permute-start.2 = (bf16[512,2048]{1,0:T(8,128)(2,1)}, bf16[512,2048]{1,0:T(8,128)(2,1)}, u32[]{:S(2)}, u32[]{:S(2)}) collective-permute-start(bf16[512,2048]{1,0:T(8,128)(2,1)} %refs_0_.3), channel_id=1, source_target_pairs={{0,2},{2,0},{1,3},{3,1},{4,6},{6,4},{5,7},{7,5},{8,10},{10,8},{9,1... | collective-permute-start | bytes 6291464 | tf_op jit(solution)/shard_map/ppermute | solution.py:349
  5.2 0.6 shard_map.163.refs_9_
  5.8 42.5 %shard_map.164 = (bf16[1024,2048]{1,0:T(8,128)(2,1)}, bf16[1024,2048]{1,0:T(8,128)(2,1)}, f32[2048,2048]{1,0:T(8,128)}, bf16[512,2048]{1,0:T(8,128)(2,1)}, bf16[...) custom-call(bf16[512,2048]{1,0:T(8,128)(2,1)} %refs_0_.3, bf16[512,2048]{1,0:T(8,128)(2,1)} %collective-permute-done.refs_1_.refs_3_, ...), custom_call_target="tpu_custom_call" | custom-call | flops 30064771072 | bytes 52428800 | tf_op jit(solution)/shard_map/pallas_call | solution.py:115
  48.3 3.5 %collective-permute-done.2.refs_0_.refs_4_ = bf16[512,2048]{1,0:T(8,128)(2,1)} collective-permute-done((bf16[512,2048]{1,0:T(8,128)(2,1)}, bf16[512,2048]{1,0:T(8,128)(2,1)}, u32[]{:S(2)}, u32[]{:S(2)}) %collective-permute-start.2) | collective-permute-done | bytes 2097184 | tf_op jit(solution)/shard_map/ppermute | solution.py:349
  51.8 1.7 collective-permute-start.7
  53.5 0.6 shard_map.165.refs_9_
  54.1 2.2 collective-permute-done.3.refs_1_.refs_5_
  56.3 38.5 %shard_map.166 = (bf16[1024,2048]{1,0:T(8,128)(2,1)}, bf16[1024,2048]{1,0:T(8,128)(2,1)}, bf16[1024,2048]{1,0:T(8,128)(2,1)}, bf16[256,2048]{1,0:T(8,128)(2,1)},...) custom-call(bf16[512,2048]{1,0:T(8,128)(2,1)} %collective-permute-done.2.refs_0_.refs_4_, ...), custom_call_target="tpu_custom_call" | custom-call | flops 25769803776 | bytes 52428800 | tf_op jit(solution)/shard_map/pallas_call | solution.py:115
  94.8 0.2 collective-permute-start.4
  94.9 0.4 collective-permute-start.9
  95.3 0.1 collective-permute-start.1
  95.4 0.4 collective-permute-start.6
  95.8 1.8 collective-permute-done.4.b
  97.7 1.3 shard_map.167.refs_7_
  99.0 1.1 collective-permute-done.7.refs_2_
  100.1 1.7 collective-permute-start.5
  101.9 1.3 shard_map.168
  103.2 0.3 collective-permute-start.10
  103.5 21.5 %shard_map.169 = f32[2048,2048]{1,0:T(8,128)} custom-call(bf16[512,2048]{1,0:T(8,128)(2,1)} %get-tuple-element.43.refs_0_, bf16[1024,2048]{1,0:T(8,128)(2,1)} %get-tuple-element.44.refs_1_.refs_2_, bf16[1024,2048]{1,0:T(8,128)(2,1)} %get-tuple-element.44.refs_1_.refs_2_, ...), custom_call_target="tpu_custom_call", output_to_operand_aliasing={{}: (6, {})} | custom-call | flops 12884901888 | bytes 33554432 | tf_op jit(solution)/shard_map/pallas_call | solution.py:153
  125.1 23.2 %collective-permute-done.10.p_far = bf16[256,2048]{1,0:T(8,128)(2,1)} collective-permute-done((bf16[256,2048]{1,0:T(8,128)(2,1)S(1)}, bf16[256,2048]{1,0:T(8,128)(2,1)}, u32[]{:S(2)}, u32[]{:S(2)}) %collective-permute-start.10) | collective-permute-done | bytes 1048608 | tf_op jit(solution)/shard_map/ppermute | solution.py:349
  148.3 4.9 %shard_map.170 = (bf16[256,2048]{1,0:T(8,128)(2,1)}, bf16[512,2048]{1,0:T(8,128)(2,1)}) custom-call(bf16[512,2048]{1,0:T(8,128)(2,1)} %get-tuple-element.33.refs_0_.p_own, bf16[512,2048]{1,0:T(8,128)(2,1)} %collective-permute-done.1.p_pair, bf16[256,2048]{1,0:T(8,128)(2,1)} %collective-permute-done.10.p_far, bf16[512,2048]{1,0:T(8,128)(2,1)} %x_in.3, ...), custom_call_target="tpu_custom_call" | custom-call | flops 1048576000 | bytes 7340032 | tf_op jit(solution)/shard_map/pallas_call | solution.py:216
  153.2 24.3 %shard_map.171 = f32[2048,2048]{1,0:T(8,128)} custom-call(bf16[512,2048]{1,0:T(8,128)(2,1)} %refs_0_.5, bf16[512,2048]{1,0:T(8,128)(2,1)} %collective-permute-done.6.refs_1_, bf16[512,2048]{1,0:T(8,128)(2,1)} %collective-permute-done.7.refs_2_, bf16[512,2048]{1,0:T(8,128)(2,1)} %collective-permute-done.8.refs_3_, ...), custom_call_target="tpu_custom_call" | custom-call | flops 17179869184 | bytes 33554432 | tf_op jit(solution)/shard_map/pallas_call | solution.py:153
  177.5 4.5 %shard_map.172 = (bf16[256,2048]{1,0:T(8,128)(2,1)}, bf16[512,2048]{1,0:T(8,128)(2,1)}) custom-call(bf16[512,2048]{1,0:T(8,128)(2,1)} %get-tuple-element.33.refs_0_.p_own, bf16[512,2048]{1,0:T(8,128)(2,1)} %collective-permute-done.1.p_pair, bf16[256,2048]{1,0:T(8,128)(2,1)S(1)} %collective-permute-done.5.p_far, ...), custom_call_target="tpu_custom_call", output_to_operand_aliasing={{1}: (6, {})} | custom-call | flops 1048576000 | bytes 7340032 | tf_op jit(solution)/shard_map/pallas_call | solution.py:216
  181.9 1.8 collective-permute-start.11
  183.7 0.3 collective-permute-start.13
  184.0 24.4 %shard_map.173.refs_5_ = f32[2048,2048]{1,0:T(8,128)} custom-call(bf16[512,2048]{1,0:T(8,128)(2,1)} %refs_0_.5, bf16[512,2048]{1,0:T(8,128)(2,1)} %collective-permute-done.6.refs_1_, bf16[512,2048]{1,0:T(8,128)(2,1)} %collective-permute-done.7.refs_2_, bf16[512,2048]{1,0:T(8,128)(2,1)} %collective-permute-done.8.refs_3_, ...), custom_call_target="tpu_custom_call" | custom-call | flops 17179869184 | bytes 33554432 | tf_op jit(solution)/shard_map/pallas_call | solution.py:153
  208.5 7.2 %shard_map.174 = (bf16[2048,512]{1,0:T(8,128)(2,1)}, f32[512,2048]{1,0:T(8,128)S(1)}) custom-call(bf16[512,2048]{1,0:T(8,128)(2,1)S(1)} %copy-done, bf16[512,2048]{1,0:T(8,128)(2,1)} %collective-permute-done.14.refs_1_, bf16[2048,512]{1,0:T(8,128)(2,1)} %refs_4_.7, bf16[2048,512]{1,0:T(8,128)(2,1)} %refs_4_.7, bf16[512,2048]{1,0:T(8,128)(2,1)} %refs_5_.5, ...), custom_call_target="tpu_custom_call" | custom-call | flops 4294967296 | bytes 8388608 | tf_op jit(solution)/shard_map/pallas_call | solution.py:273
  215.6 14.6 %collective-permute-done.13.refs_2_ = bf16[256,2048]{1,0:T(8,128)(2,1)} collective-permute-done((bf16[256,2048]{1,0:T(8,128)(2,1)}, bf16[256,2048]{1,0:T(8,128)(2,1)}, u32[]{:S(2)}, u32[]{:S(2)}) %collective-permute-start.13) | collective-permute-done | bytes 1048608 | tf_op jit(solution)/shard_map/ppermute | solution.py:349
  230.3 2.9 %collective-permute-done.15.refs_3_ = bf16[256,2048]{1,0:T(8,128)(2,1)S(1)} collective-permute-done((bf16[256,2048]{1,0:T(8,128)(2,1)}, bf16[256,2048]{1,0:T(8,128)(2,1)S(1)}, u32[]{:S(2)}, u32[]{:S(2)}) %collective-permute-start.15) | collective-permute-done | bytes 1048608 | tf_op jit(solution)/shard_map/ppermute | solution.py:352
  233.1 7.3 %shard_map.175 = (bf16[2048,512]{1,0:T(8,128)(2,1)}, f32[512,2048]{1,0:T(8,128)}) custom-call(bf16[256,2048]{1,0:T(8,128)(2,1)S(1)} %collective-permute-done.11.refs_0_, bf16[256,2048]{1,0:T(8,128)(2,1)S(1)} %collective-permute-done.12.refs_1_, bf16[256,2048]{1,0:T(8,128)(2,1)} %collective-permute-done.13.refs_2_, ...), custom_call_target="tpu_custom_call", output_to_operand_aliasing={{0}: (7, {})} | custom-call | flops 4294967296 | bytes 8388608 | tf_op jit(solution)/shard_map/pallas_call | solution.py:325
  (22 shorter events, 0.1 us)
Async XLA Ops:
  0.6 5.1 %collective-permute-start = (bf16[512,2048]{1,0:T(8,128)(2,1)}, bf16[512,2048]{1,0:T(8,128)(2,1)}, u32[]{:S(2)}, u32[]{:S(2)}) collective-permute-start(bf16[512,2048]{1,0:T(8,128)(2,1)} %refs_0_.3), channel_id=1, source_target_pairs={{0,1},{1,0},{2,3},{3,2},{4,5},{5,4},{6,7},{7,6},{8,9},{9,8},{10,11... | collective-permute-start | bytes 6291464 | tf_op jit(solution)/shard_map/ppermute | solution.py:352
  2.7 49.1 %collective-permute-start.2 = (bf16[512,2048]{1,0:T(8,128)(2,1)}, bf16[512,2048]{1,0:T(8,128)(2,1)}, u32[]{:S(2)}, u32[]{:S(2)}) collective-permute-start(bf16[512,2048]{1,0:T(8,128)(2,1)} %refs_0_.3), channel_id=1, source_target_pairs={{0,2},{2,0},{1,3},{3,1},{4,6},{6,4},{5,7},{7,5},{8,10},{10,8},{9,1... | collective-permute-start | bytes 6291464 | tf_op jit(solution)/shard_map/ppermute | solution.py:349
  51.8 4.5 %collective-permute-start.3 = (bf16[512,2048]{1,0:T(8,128)(2,1)}, bf16[512,2048]{1,0:T(8,128)(2,1)}, u32[]{:S(2)}, u32[]{:S(2)}) collective-permute-start(bf16[512,2048]{1,0:T(8,128)(2,1)} %collective-permute-done.2.refs_0_.refs_4_), channel_id=1, source_target_pairs={{0,1},{1,0},{2,3},{3,2},{4,5},{5,4},{6,7},{7,6},{8,9},{9,8},{10,11... | collective-permute-start | bytes 6291464 | tf_op jit(solution)/shard_map/ppermute | solution.py:352
  51.8 48.4 %collective-permute-start.7 = (bf16[512,2048]{1,0:T(8,128)(2,1)}, bf16[512,2048]{1,0:T(8,128)(2,1)}, u32[]{:S(2)}, u32[]{:S(2)}) collective-permute-start(bf16[512,2048]{1,0:T(8,128)(2,1)} %refs_0_.5), channel_id=1, source_target_pairs={{0,2},{2,0},{1,3},{3,1},{4,6},{6,4},{5,7},{7,5},{8,10},{10,8},{9,1... | collective-permute-start | bytes 6291464 | tf_op jit(solution)/shard_map/ppermute | solution.py:349
  94.8 2.9 %collective-permute-start.4 = (bf16[256,2048]{1,0:T(8,128)(2,1)}, bf16[256,2048]{1,0:T(8,128)(2,1)S(1)}, u32[]{:S(2)}, u32[]{:S(2)}) collective-permute-start(bf16[256,2048]{1,0:T(8,128)(2,1)} %get-tuple-element.37), channel_id=1, source_target_pairs={{0,1},{1,0},{2,3},{3,2},{4,5},{5,4},{6,7},{7,6},{8,9},{9,8},{10,11... | collective-permute-start | bytes 3145736 | tf_op jit(solution)/shard_map/ppermute | solution.py:352
  94.9 6.9 %collective-permute-start.9 = (bf16[256,2048]{1,0:T(8,128)(2,1)}, bf16[256,2048]{1,0:T(8,128)(2,1)S(1)}, u32[]{:S(2)}, u32[]{:S(2)}) collective-permute-start(bf16[256,2048]{1,0:T(8,128)(2,1)} %get-tuple-element.42), channel_id=1, source_target_pairs={{0,1},{1,0},{2,3},{3,2},{4,5},{5,4},{6,7},{7,6},{8,9},{9,8},{10,11... | collective-permute-start | bytes 3145736 | tf_op jit(solution)/shard_map/ppermute | solution.py:352
  95.3 53.0 %collective-permute-start.1 = (bf16[512,2048]{1,0:T(8,128)(2,1)}, bf16[512,2048]{1,0:T(8,128)(2,1)}, u32[]{:S(2)}, u32[]{:S(2)}) collective-permute-start(bf16[512,2048]{1,0:T(8,128)(2,1)} %get-tuple-element.34), channel_id=1, source_target_pairs={{0,1},{1,0},{2,3},{3,2},{4,5},{5,4},{6,7},{7,6},{8,9},{9,8},{10,11... | collective-permute-start | bytes 6291464 | tf_op jit(solution)/shard_map/ppermute | solution.py:352
  95.4 57.7 %collective-permute-start.6 = (bf16[512,2048]{1,0:T(8,128)(2,1)}, bf16[512,2048]{1,0:T(8,128)(2,1)}, u32[]{:S(2)}, u32[]{:S(2)}) collective-permute-start(bf16[512,2048]{1,0:T(8,128)(2,1)} %refs_0_.5), channel_id=1, source_target_pairs={{0,1},{1,0},{2,3},{3,2},{4,5},{5,4},{6,7},{7,6},{8,9},{9,8},{10,11... | collective-permute-start | bytes 6291464 | tf_op jit(solution)/shard_map/ppermute | solution.py:352
  99.0 4.5 %copy-start.2 = (bf16[256,2048]{1,0:T(8,128)(2,1)}, bf16[256,2048]{1,0:T(8,128)(2,1)S(1)}, u32[]{:S(2)}) copy-start(bf16[256,2048]{1,0:T(8,128)(2,1)S(1)} %shard_map.167.refs_7_) | copy-start | bytes 3145732
  100.1 53.0 %collective-permute-start.8 = (bf16[512,2048]{1,0:T(8,128)(2,1)}, bf16[512,2048]{1,0:T(8,128)(2,1)}, u32[]{:S(2)}, u32[]{:S(2)}) collective-permute-start(bf16[512,2048]{1,0:T(8,128)(2,1)} %collective-permute-done.7.refs_2_), channel_id=1, source_target_pairs={{0,1},{1,0},{2,3},{3,2},{4,5},{5,4},{6,7},{7,6},{8,9},{9,8},{10,11... | collective-permute-start | bytes 6291464 | tf_op jit(solution)/shard_map/ppermute | solution.py:352
  100.1 77.3 %collective-permute-start.5 = (bf16[256,2048]{1,0:T(8,128)(2,1)S(1)}, bf16[256,2048]{1,0:T(8,128)(2,1)S(1)}, u32[]{:S(2)}, u32[]{:S(2)}) collective-permute-start(bf16[256,2048]{1,0:T(8,128)(2,1)S(1)} %shard_map.167.refs_7_), channel_id=1, source_target_pairs={{0,2},{2,0},{1,3},{3,1},{4,6},{6,4},{5,7},{7,5},{8,10},{10,8},{9,1... | collective-permute-start | bytes 3145736 | tf_op jit(solution)/shard_map/ppermute | solution.py:349
  103.2 45.1 %collective-permute-start.10 = (bf16[256,2048]{1,0:T(8,128)(2,1)S(1)}, bf16[256,2048]{1,0:T(8,128)(2,1)}, u32[]{:S(2)}, u32[]{:S(2)}) collective-permute-start(bf16[256,2048]{1,0:T(8,128)(2,1)S(1)} %shard_map.168), channel_id=1, source_target_pairs={{0,2},{2,0},{1,3},{3,1},{4,6},{6,4},{5,7},{7,5},{8,10},{10,8},{9,1... | collective-permute-start | bytes 3145736 | tf_op jit(solution)/shard_map/ppermute | solution.py:349
  181.9 26.5 %collective-permute-start.14 = (bf16[512,2048]{1,0:T(8,128)(2,1)}, bf16[512,2048]{1,0:T(8,128)(2,1)}, u32[]{:S(2)}, u32[]{:S(2)}) collective-permute-start(bf16[512,2048]{1,0:T(8,128)(2,1)} %get-tuple-element.27.refs_0_), channel_id=1, source_target_pairs={{0,1},{1,0},{2,3},{3,2},{4,5},{5,4},{6,7},{7,6},{8,9},{9,8},{10,11... | collective-permute-start | bytes 6291464 | tf_op jit(solution)/shard_map/ppermute | solution.py:352
  181.9 26.5 %collective-permute-start.11 = (bf16[256,2048]{1,0:T(8,128)(2,1)}, bf16[256,2048]{1,0:T(8,128)(2,1)S(1)}, u32[]{:S(2)}, u32[]{:S(2)}) collective-permute-start(bf16[256,2048]{1,0:T(8,128)(2,1)} %get-tuple-element.47.refs_8_), channel_id=1, source_target_pairs={{0,2},{2,0},{1,3},{3,1},{4,6},{6,4},{5,7},{7,5},{8,10},{10,8},{9,1... | collective-permute-start | bytes 3145736 | tf_op jit(solution)/shard_map/ppermute | solution.py:349
  183.7 46.6 %collective-permute-start.13 = (bf16[256,2048]{1,0:T(8,128)(2,1)}, bf16[256,2048]{1,0:T(8,128)(2,1)}, u32[]{:S(2)}, u32[]{:S(2)}) collective-permute-start(bf16[256,2048]{1,0:T(8,128)(2,1)} %get-tuple-element.53.refs_8_), channel_id=1, source_target_pairs={{0,2},{2,0},{1,3},{3,1},{4,6},{6,4},{5,7},{7,5},{8,10},{10,8},{9,1... | collective-permute-start | bytes 3145736 | tf_op jit(solution)/shard_map/ppermute | solution.py:349
  184.0 24.5 %copy-start = (bf16[512,2048]{1,0:T(8,128)(2,1)S(1)}, bf16[512,2048]{1,0:T(8,128)(2,1)}, u32[]{:S(2)}) copy-start(bf16[512,2048]{1,0:T(8,128)(2,1)} %get-tuple-element.27.refs_0_) | copy-start | bytes 6291460
  208.4 24.8 %copy-start.1 = (bf16[2048,512]{1,0:T(8,128)(2,1)S(1)}, bf16[2048,512]{1,0:T(8,128)(2,1)}, u32[]{:S(2)}) copy-start(bf16[2048,512]{1,0:T(8,128)(2,1)} %refs_4_.7) | copy-start | bytes 6291460
  208.4 24.8 %copy-start.3 = (bf16[512,2048]{1,0:T(8,128)(2,1)S(1)}, bf16[512,2048]{1,0:T(8,128)(2,1)}, u32[]{:S(2)}) copy-start(bf16[512,2048]{1,0:T(8,128)(2,1)} %refs_5_.5) | copy-start | bytes 6291460
  208.4 21.9 %collective-permute-start.12 = (bf16[256,2048]{1,0:T(8,128)(2,1)S(1)}, bf16[256,2048]{1,0:T(8,128)(2,1)S(1)}, u32[]{:S(2)}, u32[]{:S(2)}) collective-permute-start(bf16[256,2048]{1,0:T(8,128)(2,1)S(1)} %collective-permute-done.11.refs_0_), channel_id=1, source_target_pairs={{0,1},{1,0},{2,3},{3,2},{4,5},{5,4},{6,7},{7,6},{8,9},{9,8},{10,11... | collective-permute-start | bytes 3145736 | tf_op jit(solution)/shard_map/ppermute | solution.py:352
  230.3 2.9 %collective-permute-start.15 = (bf16[256,2048]{1,0:T(8,128)(2,1)}, bf16[256,2048]{1,0:T(8,128)(2,1)S(1)}, u32[]{:S(2)}, u32[]{:S(2)}) collective-permute-start(bf16[256,2048]{1,0:T(8,128)(2,1)} %collective-permute-done.13.refs_2_), channel_id=1, source_target_pairs={{0,1},{1,0},{2,3},{3,2},{4,5},{5,4},{6,7},{7,6},{8,9},{9,8},{10,11... | collective-permute-start | bytes 3145736 | tf_op jit(solution)/shard_map/ppermute | solution.py:352

commit v3 on v2

--- a/solution.py
+++ b/solution.py
@@ -45,11 +45,11 @@
 
 def hidden_body(n, tiles, parts, down, *refs):
     dys, ugs, uus = refs[:n], refs[n:2 * n], refs[2 * n:3 * n]
-    wd, wg, wu = refs[3 * n:3 * n + 3]
+    wd, wg_all, wu_all = refs[3 * n:3 * n + 3]
     m = n * parts
-    outs = refs[-(m + 5 + (down > 0) + (down < n)):-(m + 3)]
+    outs = refs[-(m + 8 + (down > 0) + (down < n)):-(m + 6)]
     dg, du = outs[:2]
-    ps, (acc, held_g, held_u) = refs[-(m + 3):-3], refs[-3:]
+    ps, (acc, held_g, held_u, wg, wu, sems) = refs[-(m + 6):-6], refs[-6:]
     step = pl.program_id(0)
     rows = dys[0].shape[0]
     piece = rows // parts
@@ -78,22 +78,38 @@
         if down:
             outs[2][...] = total
 
+    def fetch(k, slot):
+        cols = pl.ds(pl.multiple_of(k * tile, tile), tile)
+        return [pltpu.make_async_copy(wg_all.at[:, cols], wg.at[slot], sems.at[0, slot]),
+                pltpu.make_async_copy(wu_all.at[:, cols], wu.at[slot], sems.at[1, slot])]
+
     def term(slot):
-        return dot(held_g[slot], wg[...], COLS_T) + dot(held_u[slot], wu[...], COLS_T)
+        return dot(held_g[slot], wg[slot], COLS_T) + dot(held_u[slot], wu[slot], COLS_T)
+
+    tile = wd.shape[0]
 
     @pl.when(step == 0)
     def _():
+        for c in fetch(0, 0):
+            c.start()
         form(0)
 
     @pl.when((step > 0) & (step < tiles))
     def _():
         slot = lax.rem(step, 2)
+        for c in fetch(step, slot):
+            c.start()
+        for c in fetch(step - 1, 1 - slot):
+            c.wait()
         acc[...] = jnp.where(step == 1, 0.0, acc[...]) + term(1 - slot)
         form(slot)
 
     @pl.when(step == tiles)
     def _():
-        total = acc[...] + term((tiles - 1) % 2)
+        last = (tiles - 1) % 2
+        for c in fetch(tiles - 1, last):
+            c.wait()
+        total = acc[...] + term(last)
         for i in range(m):
             ps[i][...] = total[i * piece:(i + 1) * piece].astype(BF16)
 
@@ -104,23 +120,22 @@
     cols = w_down.shape[0]
     tiles = cols // tile
     now = lambda s: jnp.minimum(s, tiles - 1)
-    before = lambda s: jnp.maximum(s - 1, 0)
     u_specs = [pl.BlockSpec((rows, tile), functools.partial(lambda k, s: (block_of(k), now(s)), k)) for k in blocks]
     tile_out = pl.BlockSpec((n * rows, tile), lambda s: (0, now(s)))
     z_out = pl.BlockSpec(((n - down) * rows, tile), lambda s: (0, now(s)))
-    w_late = pl.BlockSpec((width, tile), lambda s: (0, before(s)))
     w_now = pl.BlockSpec((tile, width), lambda s: (now(s), 0))
     wide = jax.ShapeDtypeStruct((n * rows, cols), BF16)
     piece = (rows // parts, width)
     return pl.pallas_call(
         functools.partial(hidden_body, n, tiles, parts, down),
         grid=(tiles + 1,),
-        in_specs=[once((rows, width))] * n + u_specs + u_specs + [w_now, w_late, w_late] + [ANY] * len(deps),
+        in_specs=[once((rows, width))] * n + u_specs + u_specs + [w_now, ANY, ANY] + [ANY] * len(deps),
         out_specs=[tile_out] * 2 + [w_now] * (down > 0) + [z_out] * (down < n) + [once(piece)] * (n * parts),
         out_shape=[wide] * 2 + [jax.ShapeDtypeStruct((cols, width), F32)] * (down > 0)
         + [jax.ShapeDtypeStruct(((n - down) * rows, cols), BF16)] * (down < n)
         + [jax.ShapeDtypeStruct(piece, BF16)] * (n * parts),
-        scratch_shapes=[pltpu.VMEM((n * rows, width), F32)] + [pltpu.VMEM((2, n * rows, tile), BF16)] * 2,
+        scratch_shapes=[pltpu.VMEM((n * rows, width), F32)] + [pltpu.VMEM((2, n * rows, tile), BF16)] * 2
+        + [pltpu.VMEM((2, width, tile), BF16)] * 2 + [pltpu.SemaphoreType.DMA((2, 2))],
         compiler_params=params(),
         cost_estimate=pl.CostEstimate(flops=(6 * n + 2 * down) * rows * width * cols, bytes_accessed=50 << 20,
                                       transcendentals=n * rows * cols),
@@ -143,7 +158,7 @@
     out[...] = total
 
 
-def weight_grad(lefts, rights, prev=None, deps=(), tm=256):
+def weight_grad(lefts, rights, prev=None, deps=(), tm=256, limit=VMEM_LIMIT):
     n = len(lefts)
     m, cols = lefts[0][0].shape[1], rights[0][0].shape[1]
     l_specs = [pl.BlockSpec((BLOCK, tm), functools.partial(lambda b, i: (b, i), b)) for _, b in lefts]
@@ -157,7 +172,7 @@
         out_specs=out_spec,
         out_shape=jax.ShapeDtypeStruct((m, cols), F32),
         input_output_aliases={2 * n: 0} if more else {},
-        compiler_params=params(),
+        compiler_params=params(limit),
         cost_estimate=pl.CostEstimate(flops=2 * n * BLOCK * m * cols, bytes_accessed=32 << 20, transcendentals=0),
     )(*hbm(*[a for a, _ in lefts], *[a for a, _ in rights], *more, *deps))
 
@@ -225,68 +240,9 @@
     )(*hbm(p_own, p_pair), p_far, *hbm(x_in, grad_res, gamma, *extra))
 
 
-def proj_body(places, first, *refs):
+def proj_body(places, tile, more, *refs):
     n = len(places)
-    ds, o, w_out = refs[:n], refs[n:2 * n], refs[2 * n]
-    grad_o, grad_w, acc, stage, sem = refs[-5:]
-    step = pl.program_id(0)
-    spans, at = [], 0
-    for r in ds:
-        spans.append(pl.ds(at, r.shape[0]))
-        at += r.shape[0]
-
-    @pl.when(step == 0)
-    def _():
-        acc[...] = jnp.zeros_like(acc)
-
-    total = dot(o[0][...], ds[0][...], ROWS_T)
-    for i in range(n):
-        acc[spans[i], :] += dot(ds[i][...], w_out[...], COLS_T)
-        if i:
-            total += dot(o[i][...], ds[i][...], ROWS_T)
-    grad_w[...] = total if first else refs[2 * n + 1][...] + total
-
-    @pl.when(step == pl.num_programs(0) - 1)
-    def _():
-        stage[...] = acc[...].astype(BF16)
-        copies = []
-        for i, (k, start) in enumerate(places):
-            rows = ds[i].shape[0]
-            to = pl.ds(pl.multiple_of(block_of(k) * BLOCK + start, rows), rows)
-            copies.append(pltpu.make_async_copy(stage.at[spans[i], :], grad_o.at[to, :], sem.at[i]))
-        for c in copies:
-            c.start()
-        for c in copies:
-            c.wait()
-
-
-def out_proj(pieces, attn_out, w_out, prev, deps=(), tile=512):
-    n = len(pieces)
-    tokens, cols = attn_out.shape
-    width = w_out.shape[1]
-    sizes = [a.shape[0] for a, _, _ in pieces]
-    places = [(k, start) for _, k, start in pieces]
-    o_specs = [once((r, cols), functools.partial(lambda k, r, start, h: ((block_of(k) * BLOCK + start) // r, 0), k, r, start))
-               for r, (k, start) in zip(sizes, places)]
-    w_spec = pl.BlockSpec((cols, tile), lambda h: (0, h))
-    first = prev is None
-    return pl.pallas_call(
-        functools.partial(proj_body, places, first),
-        grid=(width // tile,),
-        in_specs=[pl.BlockSpec((r, tile), lambda h: (0, h)) for r in sizes] + o_specs + [w_spec]
-        + ([] if first else [w_spec, ANY]) + [ANY] * len(deps),
-        out_specs=[ANY, w_spec],
-        out_shape=[jax.ShapeDtypeStruct((tokens, cols), BF16), jax.ShapeDtypeStruct((cols, width), F32)],
-        scratch_shapes=[pltpu.VMEM((sum(sizes), cols), F32), pltpu.VMEM((sum(sizes), cols), BF16), pltpu.SemaphoreType.DMA((n,))],
-        input_output_aliases={} if first else {2 * n + 1: 1, 2 * n + 2: 0},
-        compiler_params=params(24 << 20),
-        cost_estimate=pl.CostEstimate(flops=4 * sum(sizes) * width * cols, bytes_accessed=8 << 20, transcendentals=0),
-    )(*[a for a, _, _ in pieces], *hbm(*[attn_out] * n, w_out, *([] if first else [prev[1], prev[0]]), *deps))
-
-
-def last_body(places, tile, *refs):
-    n = len(places)
-    ds, (o, w_out, prev_w) = refs[:n], refs[n:n + 3]
+    ds, (o, w_out) = refs[:n], refs[n:n + 2]
     grad_o, grad_w, held, stage, sem_w, sem_o = refs[-6:]
     rows = ds[0].shape[0]
     tiles = w_out.shape[1] // tile
@@ -305,7 +261,7 @@
         total = dot(o[o_rows[0], :], ds[0][:, cols], ROWS_T)
         for i in range(1, n):
             total += dot(o[o_rows[i], :], ds[i][:, cols], ROWS_T)
-        held[:, cols] = total + prev_w[:, cols]
+        held[:, cols] = total + refs[n + 2][:, cols] if more else total
         w_copy(h).start()
 
     for i in range(n):
@@ -317,22 +273,24 @@
         w_copy(h).wait()
 
 
-def last_proj(pieces, attn_out, w_out, prev, tile=512):
+def out_proj(pieces, attn_out, w_out, prev=None, deps=(), tile=1024):
     n = len(pieces)
     tokens, cols = attn_out.shape
     width = w_out.shape[1]
     rows = pieces[0][0].shape[0]
-    return pl.pallas_call(
-        functools.partial(last_body, [(k, start) for _, k, start in pieces], tile),
-        in_specs=[pl.BlockSpec(memory_space=pltpu.VMEM)] * (n + 3) + [ANY],
+    vmem = pl.BlockSpec(memory_space=pltpu.VMEM)
+    more = prev is not None
+    return pl.pallas_call(
+        functools.partial(proj_body, [(k, start) for _, k, start in pieces], tile, more),
+        in_specs=[vmem] * (n + 2) + ([vmem, ANY] if more else []) + [ANY] * len(deps),
         out_specs=[ANY, ANY],
         out_shape=[jax.ShapeDtypeStruct((tokens, cols), BF16), jax.ShapeDtypeStruct((cols, width), F32)],
         scratch_shapes=[pltpu.VMEM((cols, width), F32), pltpu.VMEM((n * rows, cols), BF16),
                         pltpu.SemaphoreType.DMA((width // tile,)), pltpu.SemaphoreType.DMA((n,))],
-        input_output_aliases={n + 3: 0},
+        input_output_aliases={n + 3: 0} if more else {},
         compiler_params=params(16 << 20),
         cost_estimate=pl.CostEstimate(flops=4 * n * rows * width * cols, bytes_accessed=8 << 20, transcendentals=0),
-    )(*[a for a, _, _ in pieces], attn_out, w_out, prev[1], *hbm(prev[0]))
+    )(*[a for a, _, _ in pieces], attn_out, w_out, *([prev[1], *hbm(prev[0])] if more else []), *hbm(*deps))
 
 
 DX_PARTS = 2
@@ -381,7 +339,7 @@
 
         xs = [(x_norm, 0), (x_sib, 0), (x_far, 0), (x_diag, 0)]
         rest = [functools.partial(weight_grad, xs, [(dg_near, 0), (dg_near, 1), (dg_far, 0), (dg_far, 1)]),
-                functools.partial(weight_grad, xs, [(du_near, 0), (du_near, 1), (du_far, 0), (du_far, 1)])]
+                functools.partial(weight_grad, xs, [(du_near, 0), (du_near, 1), (du_far, 0), (du_far, 1)], limit=48 << 20)]
         dx_rows = BLOCK // DX_PARTS
         whole, fars, places, grads, at, prev = None, [], [], [], 0, gw_down
         for c, n in enumerate(DS_PIECES):
@@ -397,13 +355,13 @@
             at += n
         gw_gate, gw_up = grads
         sib = pair(whole)
-        near = out_proj([(whole, OWN, 0), (sib, SIB, 0)], attn_out, w_out, None, deps=(gw_up,), tile=2048)
+        near = out_proj([(whole, OWN, 0), (sib, SIB, 0)], attn_out, w_out, deps=(gw_up,))
         pieces, prev = [], gw_up
         for c, at in enumerate(places):
             far = after(fars[c], prev)
             pieces += [(far, FAR, at), (pair(far), DIAG, at)]
             prev = near[1]
-        grad_attn, gw_out = last_proj(pieces, attn_out, w_out, near)
+        grad_attn, gw_out = out_proj(pieces, attn_out, w_out, near)
         return whole, grad_attn, gw_gate, gw_up, gw_down, gw_out
 
 

time: 241 us -> 240 us (level)
  Pallas kernels: 179 us -> 175 us
where the time goes in v3:
time: 240 us; the launch traced here: 239 us
  Pallas kernels  175 us (73%)
  waiting for transfers between devices  50.9 us (21%)
  starting transfers between devices  10.2 us (4%)
    pallas_call x2, Pallas kernels, hidden(): pl.pallas_call(functools.partial(hidden_body, n, tiles, parts, down), gri...  79.3 us
    pallas_call x3, Pallas kernels, weight_grad(): pl.pallas_call(functools.partial(grad_body if prev is None else grad_more...  70.2 us
    ppermute x6, waiting for transfers between devices, cross(): return lax.ppermute(a, 'tp', CROSS)  44.2 us
    pallas_call x2, Pallas kernels, out_proj(): pl.pallas_call(functools.partial(proj_body, [(k, start) for _, k, start i...  12.4 us
    pallas_call x2, Pallas kernels, norm_backward(): pl.pallas_call(norm_body, grid=(rows // tile,), in_specs=[here, here, rec...  9.3 us
    ppermute x6, starting transfers between devices, cross(): return lax.ppermute(a, 'tp', CROSS)  8.36 us
    ppermute x10, waiting for transfers between devices, pair(): return lax.ppermute(a, 'tp', PAIR)  6.68 us
  transfers between devices with their start and end apart: 16, of which 7 were waited for; matrix products, arithmetic and copies ran while one was open for 1% of the time, Pallas kernels for 69%

profile of v3, /device:TPU:0, one launch (start us, length us, event | category | flops | bytes accessed | tf_op | source)
XLA Modules:
  0.0 239.4 jit_solution(1519211033639404211)
XLA Ops:
  0.6 0.8 collective-permute-start
  1.4 1.3 reshape.15.refs_0_.gamma
  2.7 2.5 %collective-permute-start.2 = (bf16[512,2048]{1,0:T(8,128)(2,1)}, bf16[512,2048]{1,0:T(8,128)(2,1)}, u32[]{:S(2)}, u32[]{:S(2)}) collective-permute-start(bf16[512,2048]{1,0:T(8,128)(2,1)} %refs_0_.3), channel_id=1, source_target_pairs={{0,2},{2,0},{1,3},{3,1},{4,6},{6,4},{5,7},{7,5},{8,10},{10,8},{9,1... | collective-permute-start | bytes 6291464 | tf_op jit(solution)/shard_map/ppermute | solution.py:307
  5.2 0.6 shard_map.163.refs_9_
  5.8 41.8 %shard_map.164 = (bf16[1024,2048]{1,0:T(8,128)(2,1)}, bf16[1024,2048]{1,0:T(8,128)(2,1)}, f32[2048,2048]{1,0:T(8,128)}, bf16[512,2048]{1,0:T(8,128)(2,1)}, bf16[...) custom-call(bf16[512,2048]{1,0:T(8,128)(2,1)} %refs_0_.3, bf16[512,2048]{1,0:T(8,128)(2,1)} %collective-permute-done.refs_1_.refs_3_, ...), custom_call_target="tpu_custom_call" | custom-call | flops 30064771072 | bytes 52428800 | tf_op jit(solution)/shard_map/pallas_call | solution.py:129
  47.6 4.2 %collective-permute-done.2.refs_0_.refs_4_ = bf16[512,2048]{1,0:T(8,128)(2,1)} collective-permute-done((bf16[512,2048]{1,0:T(8,128)(2,1)}, bf16[512,2048]{1,0:T(8,128)(2,1)}, u32[]{:S(2)}, u32[]{:S(2)}) %collective-permute-start.2) | collective-permute-done | bytes 2097184 | tf_op jit(solution)/shard_map/ppermute | solution.py:307
  51.8 1.7 collective-permute-start.7
  53.5 0.6 shard_map.165.refs_9_
  54.1 2.2 collective-permute-done.3.refs_1_.refs_5_
  56.3 37.5 %shard_map.166 = (bf16[1024,2048]{1,0:T(8,128)(2,1)}, bf16[1024,2048]{1,0:T(8,128)(2,1)}, bf16[1024,2048]{1,0:T(8,128)(2,1)}, bf16[256,2048]{1,0:T(8,128)(2,1)},...) custom-call(bf16[512,2048]{1,0:T(8,128)(2,1)} %collective-permute-done.2.refs_0_.refs_4_, ...), custom_call_target="tpu_custom_call" | custom-call | flops 25769803776 | bytes 52428800 | tf_op jit(solution)/shard_map/pallas_call | solution.py:129
  93.8 0.1 collective-permute-start.4
  93.9 0.4 collective-permute-start.9
  94.4 0.4 collective-permute-start.6
  94.8 1.8 collective-permute-done.4.b
  96.7 1.3 shard_map.167.refs_7_
  98.0 2.1 collective-permute-done.7.refs_2_
  100.1 1.7 collective-permute-start.5
  101.9 1.3 shard_map.168
  103.2 0.3 collective-permute-start.10
  103.5 21.5 %shard_map.169 = f32[2048,2048]{1,0:T(8,128)} custom-call(bf16[512,2048]{1,0:T(8,128)(2,1)} %get-tuple-element.43.refs_0_, bf16[1024,2048]{1,0:T(8,128)(2,1)} %get-tuple-element.44.refs_1_.refs_2_, bf16[1024,2048]{1,0:T(8,128)(2,1)} %get-tuple-element.44.refs_1_.refs_2_, ...), custom_call_target="tpu_custom_call", output_to_operand_aliasing={{}: (6, {})} | custom-call | flops 12884901888 | bytes 33554432 | tf_op jit(solution)/shard_map/pallas_call | solution.py:168
  125.1 23.2 %collective-permute-done.10.p_far = bf16[256,2048]{1,0:T(8,128)(2,1)} collective-permute-done((bf16[256,2048]{1,0:T(8,128)(2,1)S(1)}, bf16[256,2048]{1,0:T(8,128)(2,1)}, u32[]{:S(2)}, u32[]{:S(2)}) %collective-permute-start.10) | collective-permute-done | bytes 1048608 | tf_op jit(solution)/shard_map/ppermute | solution.py:307
  148.3 4.8 %shard_map.170 = (bf16[256,2048]{1,0:T(8,128)(2,1)S(1)}, bf16[512,2048]{1,0:T(8,128)(2,1)}) custom-call(bf16[512,2048]{1,0:T(8,128)(2,1)} %get-tuple-element.33.refs_0_.p_own, bf16[512,2048]{1,0:T(8,128)(2,1)} %collective-permute-done.1.p_pair, bf16[256,2048]{1,0:T(8,128)(2,1)} %collective-permute-done.10.p_far, bf16[512,2048]{1,0:T(8,128)(2,1)} %x_in.3, ...), custom_call_target="tpu_custom_call" | custom-call | flops 1048576000 | bytes 7340032 | tf_op jit(solution)/shard_map/pallas_call | solution.py:231
  153.1 1.0 copy-done.4
  154.1 24.3 %shard_map.171 = f32[2048,2048]{1,0:T(8,128)} custom-call(bf16[512,2048]{1,0:T(8,128)(2,1)} %refs_0_.5, bf16[512,2048]{1,0:T(8,128)(2,1)} %collective-permute-done.6.refs_1_, bf16[512,2048]{1,0:T(8,128)(2,1)} %collective-permute-done.7.refs_2_, bf16[512,2048]{1,0:T(8,128)(2,1)} %collective-permute-done.8.refs_3_, ...), custom_call_target="tpu_custom_call" | custom-call | flops 17179869184 | bytes 33554432 | tf_op jit(solution)/shard_map/pallas_call | solution.py:168
  178.4 4.5 %shard_map.172 = (bf16[256,2048]{1,0:T(8,128)(2,1)S(1)}, bf16[512,2048]{1,0:T(8,128)(2,1)}) custom-call(bf16[512,2048]{1,0:T(8,128)(2,1)} %get-tuple-element.33.refs_0_.p_own, bf16[512,2048]{1,0:T(8,128)(2,1)} %collective-permute-done.1.p_pair, bf16[256,2048]{1,0:T(8,128)(2,1)S(1)} %collective-permute-done.5.p_far, ...), custom_call_target="tpu_custom_call", output_to_operand_aliasing={{1}: (6, {})} | custom-call | flops 1048576000 | bytes 7340032 | tf_op jit(solution)/shard_map/pallas_call | solution.py:231
  182.9 1.8 collective-permute-start.11
  184.7 0.3 collective-permute-start.13
  184.9 24.4 %shard_map.173.refs_4_ = f32[2048,2048]{1,0:T(8,128)} custom-call(bf16[512,2048]{1,0:T(8,128)(2,1)} %refs_0_.5, bf16[512,2048]{1,0:T(8,128)(2,1)} %collective-permute-done.6.refs_1_, bf16[512,2048]{1,0:T(8,128)(2,1)} %collective-permute-done.7.refs_2_, bf16[512,2048]{1,0:T(8,128)(2,1)} %collective-permute-done.8.refs_3_, ...), custom_call_target="tpu_custom_call" | custom-call | flops 17179869184 | bytes 33554432 | tf_op jit(solution)/shard_map/pallas_call | solution.py:168
  209.4 6.8 %shard_map.174 = (bf16[2048,512]{1,0:T(8,128)(2,1)}, f32[512,2048]{1,0:T(8,128)S(1)}) custom-call(bf16[512,2048]{1,0:T(8,128)(2,1)S(1)} %copy-done, bf16[512,2048]{1,0:T(8,128)(2,1)S(1)} %collective-permute-done.14.refs_1_, bf16[2048,512]{1,0:T(8,128)(2,1)S(1)} %copy-done.2, bf16[512,2048]{1,0:T(8,128)(2,1)S(1)} %copy-done.3, f32[2048,2048]{1,0:T(8,128)} %shard_map.173.refs_4_), custom_call_target="tpu_custom_call" | custom-call | flops 4294967296 | bytes 8388608 | tf_op jit(solution)/shard_map/pallas_call | solution.py:283
  216.2 14.7 %collective-permute-done.13.refs_2_ = bf16[256,2048]{1,0:T(8,128)(2,1)S(1)} collective-permute-done((bf16[256,2048]{1,0:T(8,128)(2,1)S(1)}, bf16[256,2048]{1,0:T(8,128)(2,1)S(1)}, u32[]{:S(2)}, u32[]{:S(2)}) %collective-permute-start.13) | collective-permute-done | bytes 1048608 | tf_op jit(solution)/shard_map/ppermute | solution.py:307
  230.9 2.7 %collective-permute-done.15.refs_3_ = bf16[256,2048]{1,0:T(8,128)(2,1)S(1)} collective-permute-done((bf16[256,2048]{1,0:T(8,128)(2,1)S(1)}, bf16[256,2048]{1,0:T(8,128)(2,1)S(1)}, u32[]{:S(2)}, u32[]{:S(2)}) %collective-permute-start.15) | collective-permute-done | bytes 1048608 | tf_op jit(solution)/shard_map/ppermute | solution.py:310
  233.6 5.7 %shard_map.175 = (bf16[2048,512]{1,0:T(8,128)(2,1)}, f32[512,2048]{1,0:T(8,128)}) custom-call(bf16[256,2048]{1,0:T(8,128)(2,1)S(1)} %collective-permute-done.11.refs_0_, bf16[256,2048]{1,0:T(8,128)(2,1)S(1)} %collective-permute-done.12.refs_1_, bf16[256,2048]{1,0:T(8,128)(2,1)S(1)} %collective-permute-done.13.refs_2_, ...), custom_call_target="tpu_custom_call", output_to_operand_aliasing={{0}: (7, {})} | custom-call | flops 4294967296 | bytes 8388608 | tf_op jit(solution)/shard_map/pallas_call | solution.py:283
  (28 shorter events, 0.2 us)
Async XLA Ops:
  0.6 5.1 %collective-permute-start = (bf16[512,2048]{1,0:T(8,128)(2,1)}, bf16[512,2048]{1,0:T(8,128)(2,1)}, u32[]{:S(2)}, u32[]{:S(2)}) collective-permute-start(bf16[512,2048]{1,0:T(8,128)(2,1)} %refs_0_.3), channel_id=1, source_target_pairs={{0,1},{1,0},{2,3},{3,2},{4,5},{5,4},{6,7},{7,6},{8,9},{9,8},{10,11... | collective-permute-start | bytes 6291464 | tf_op jit(solution)/shard_map/ppermute | solution.py:310
  2.7 49.1 %collective-permute-start.2 = (bf16[512,2048]{1,0:T(8,128)(2,1)}, bf16[512,2048]{1,0:T(8,128)(2,1)}, u32[]{:S(2)}, u32[]{:S(2)}) collective-permute-start(bf16[512,2048]{1,0:T(8,128)(2,1)} %refs_0_.3), channel_id=1, source_target_pairs={{0,2},{2,0},{1,3},{3,1},{4,6},{6,4},{5,7},{7,5},{8,10},{10,8},{9,1... | collective-permute-start | bytes 6291464 | tf_op jit(solution)/shard_map/ppermute | solution.py:307
  51.8 4.5 %collective-permute-start.3 = (bf16[512,2048]{1,0:T(8,128)(2,1)}, bf16[512,2048]{1,0:T(8,128)(2,1)}, u32[]{:S(2)}, u32[]{:S(2)}) collective-permute-start(bf16[512,2048]{1,0:T(8,128)(2,1)} %collective-permute-done.2.refs_0_.refs_4_), channel_id=1, source_target_pairs={{0,1},{1,0},{2,3},{3,2},{4,5},{5,4},{6,7},{7,6},{8,9},{9,8},{10,11... | collective-permute-start | bytes 6291464 | tf_op jit(solution)/shard_map/ppermute | solution.py:310
  51.8 48.4 %collective-permute-start.7 = (bf16[512,2048]{1,0:T(8,128)(2,1)}, bf16[512,2048]{1,0:T(8,128)(2,1)}, u32[]{:S(2)}, u32[]{:S(2)}) collective-permute-start(bf16[512,2048]{1,0:T(8,128)(2,1)} %refs_0_.5), channel_id=1, source_target_pairs={{0,2},{2,0},{1,3},{3,1},{4,6},{6,4},{5,7},{7,5},{8,10},{10,8},{9,1... | collective-permute-start | bytes 6291464 | tf_op jit(solution)/shard_map/ppermute | solution.py:307
  93.8 2.9 %collective-permute-start.4 = (bf16[256,2048]{1,0:T(8,128)(2,1)}, bf16[256,2048]{1,0:T(8,128)(2,1)S(1)}, u32[]{:S(2)}, u32[]{:S(2)}) collective-permute-start(bf16[256,2048]{1,0:T(8,128)(2,1)} %get-tuple-element.37), channel_id=1, source_target_pairs={{0,1},{1,0},{2,3},{3,2},{4,5},{5,4},{6,7},{7,6},{8,9},{9,8},{10,11... | collective-permute-start | bytes 3145736 | tf_op jit(solution)/shard_map/ppermute | solution.py:310
  93.9 8.0 %collective-permute-start.9 = (bf16[256,2048]{1,0:T(8,128)(2,1)}, bf16[256,2048]{1,0:T(8,128)(2,1)S(1)}, u32[]{:S(2)}, u32[]{:S(2)}) collective-permute-start(bf16[256,2048]{1,0:T(8,128)(2,1)} %get-tuple-element.42), channel_id=1, source_target_pairs={{0,1},{1,0},{2,3},{3,2},{4,5},{5,4},{6,7},{7,6},{8,9},{9,8},{10,11... | collective-permute-start | bytes 3145736 | tf_op jit(solution)/shard_map/ppermute | solution.py:310
  94.3 54.0 %collective-permute-start.1 = (bf16[512,2048]{1,0:T(8,128)(2,1)}, bf16[512,2048]{1,0:T(8,128)(2,1)}, u32[]{:S(2)}, u32[]{:S(2)}) collective-permute-start(bf16[512,2048]{1,0:T(8,128)(2,1)} %get-tuple-element.34), channel_id=1, source_target_pairs={{0,1},{1,0},{2,3},{3,2},{4,5},{5,4},{6,7},{7,6},{8,9},{9,8},{10,11... | collective-permute-start | bytes 6291464 | tf_op jit(solution)/shard_map/ppermute | solution.py:310
  94.4 59.7 %collective-permute-start.6 = (bf16[512,2048]{1,0:T(8,128)(2,1)}, bf16[512,2048]{1,0:T(8,128)(2,1)}, u32[]{:S(2)}, u32[]{:S(2)}) collective-permute-start(bf16[512,2048]{1,0:T(8,128)(2,1)} %refs_0_.5), channel_id=1, source_target_pairs={{0,1},{1,0},{2,3},{3,2},{4,5},{5,4},{6,7},{7,6},{8,9},{9,8},{10,11... | collective-permute-start | bytes 6291464 | tf_op jit(solution)/shard_map/ppermute | solution.py:310
  98.0 5.5 %copy-start.1 = (bf16[256,2048]{1,0:T(8,128)(2,1)}, bf16[256,2048]{1,0:T(8,128)(2,1)S(1)}, u32[]{:S(2)}) copy-start(bf16[256,2048]{1,0:T(8,128)(2,1)S(1)} %shard_map.167.refs_7_) | copy-start | bytes 3145732
  100.1 53.9 %collective-permute-start.8 = (bf16[512,2048]{1,0:T(8,128)(2,1)}, bf16[512,2048]{1,0:T(8,128)(2,1)}, u32[]{:S(2)}, u32[]{:S(2)}) collective-permute-start(bf16[512,2048]{1,0:T(8,128)(2,1)} %collective-permute-done.7.refs_2_), channel_id=1, source_target_pairs={{0,1},{1,0},{2,3},{3,2},{4,5},{5,4},{6,7},{7,6},{8,9},{9,8},{10,11... | collective-permute-start | bytes 6291464 | tf_op jit(solution)/shard_map/ppermute | solution.py:310
  100.1 78.2 %collective-permute-start.5 = (bf16[256,2048]{1,0:T(8,128)(2,1)S(1)}, bf16[256,2048]{1,0:T(8,128)(2,1)S(1)}, u32[]{:S(2)}, u32[]{:S(2)}) collective-permute-start(bf16[256,2048]{1,0:T(8,128)(2,1)S(1)} %shard_map.167.refs_7_), channel_id=1, source_target_pairs={{0,2},{2,0},{1,3},{3,1},{4,6},{6,4},{5,7},{7,5},{8,10},{10,8},{9,1... | collective-permute-start | bytes 3145736 | tf_op jit(solution)/shard_map/ppermute | solution.py:307
  103.2 45.1 %collective-permute-start.10 = (bf16[256,2048]{1,0:T(8,128)(2,1)S(1)}, bf16[256,2048]{1,0:T(8,128)(2,1)}, u32[]{:S(2)}, u32[]{:S(2)}) collective-permute-start(bf16[256,2048]{1,0:T(8,128)(2,1)S(1)} %shard_map.168), channel_id=1, source_target_pairs={{0,2},{2,0},{1,3},{3,1},{4,6},{6,4},{5,7},{7,5},{8,10},{10,8},{9,1... | collective-permute-start | bytes 3145736 | tf_op jit(solution)/shard_map/ppermute | solution.py:307
  153.1 1.0 copy-start.4
  178.4 4.5 %copy-start.5 = (bf16[256,2048]{1,0:T(8,128)(2,1)S(1)}, bf16[256,2048]{1,0:T(8,128)(2,1)}, u32[]{:S(2)}) copy-start(bf16[256,2048]{1,0:T(8,128)(2,1)} %copy-done.4) | copy-start | bytes 3145732
  182.9 2.1 copy-start.6
  182.9 26.5 %collective-permute-start.14 = (bf16[512,2048]{1,0:T(8,128)(2,1)}, bf16[512,2048]{1,0:T(8,128)(2,1)S(1)}, u32[]{:S(2)}, u32[]{:S(2)}) collective-permute-start(bf16[512,2048]{1,0:T(8,128)(2,1)} %get-tuple-element.27.refs_0_), channel_id=1, source_target_pairs={{0,1},{1,0},{2,3},{3,2},{4,5},{5,4},{6,7},{7,6},{8,9},{9,8},{10,11... | collective-permute-start | bytes 6291464 | tf_op jit(solution)/shard_map/ppermute | solution.py:310
  182.9 26.5 %collective-permute-start.11 = (bf16[256,2048]{1,0:T(8,128)(2,1)S(1)}, bf16[256,2048]{1,0:T(8,128)(2,1)S(1)}, u32[]{:S(2)}, u32[]{:S(2)}) collective-permute-start(bf16[256,2048]{1,0:T(8,128)(2,1)S(1)} %copy-done.5), channel_id=1, source_target_pairs={{0,2},{2,0},{1,3},{3,1},{4,6},{6,4},{5,7},{7,5},{8,10},{10,8},{9,1... | collective-permute-start | bytes 3145736 | tf_op jit(solution)/shard_map/ppermute | solution.py:307
  184.7 46.3 %collective-permute-start.13 = (bf16[256,2048]{1,0:T(8,128)(2,1)S(1)}, bf16[256,2048]{1,0:T(8,128)(2,1)S(1)}, u32[]{:S(2)}, u32[]{:S(2)}) collective-permute-start(bf16[256,2048]{1,0:T(8,128)(2,1)S(1)} %get-tuple-element.53.refs_8_), channel_id=1, source_target_pairs={{0,2},{2,0},{1,3},{3,1},{4,6},{6,4},{5,7},{7,5},{8,10},{10,8},{9,1... | collective-permute-start | bytes 3145736 | tf_op jit(solution)/shard_map/ppermute | solution.py:307
  184.9 24.5 %copy-start = (bf16[512,2048]{1,0:T(8,128)(2,1)S(1)}, bf16[512,2048]{1,0:T(8,128)(2,1)}, u32[]{:S(2)}) copy-start(bf16[512,2048]{1,0:T(8,128)(2,1)} %get-tuple-element.27.refs_0_) | copy-start | bytes 6291460
  184.9 24.5 %copy-start.2 = (bf16[2048,512]{1,0:T(8,128)(2,1)S(1)}, bf16[2048,512]{1,0:T(8,128)(2,1)}, u32[]{:S(2)}) copy-start(bf16[2048,512]{1,0:T(8,128)(2,1)} %refs_4_.5) | copy-start | bytes 6291460
  184.9 24.5 %copy-start.3 = (bf16[512,2048]{1,0:T(8,128)(2,1)S(1)}, bf16[512,2048]{1,0:T(8,128)(2,1)}, u32[]{:S(2)}) copy-start(bf16[512,2048]{1,0:T(8,128)(2,1)} %refs_5_.5) | copy-start | bytes 6291460
  209.3 21.6 %collective-permute-start.12 = (bf16[256,2048]{1,0:T(8,128)(2,1)S(1)}, bf16[256,2048]{1,0:T(8,128)(2,1)S(1)}, u32[]{:S(2)}, u32[]{:S(2)}) collective-permute-start(bf16[256,2048]{1,0:T(8,128)(2,1)S(1)} %collective-permute-done.11.refs_0_), channel_id=1, source_target_pairs={{0,1},{1,0},{2,3},{3,2},{4,5},{5,4},{6,7},{7,6},{8,9},{9,8},{10,11... | collective-permute-start | bytes 3145736 | tf_op jit(solution)/shard_map/ppermute | solution.py:310
  230.9 2.7 %collective-permute-start.15 = (bf16[256,2048]{1,0:T(8,128)(2,1)S(1)}, bf16[256,2048]{1,0:T(8,128)(2,1)S(1)}, u32[]{:S(2)}, u32[]{:S(2)}) collective-permute-start(bf16[256,2048]{1,0:T(8,128)(2,1)S(1)} %collective-permute-done.13.refs_2_), channel_id=1, source_target_pairs={{0,1},{1,0},{2,3},{3,2},{4,5},{5,4},{6,7},{7,6},{8,9},{9,8},{10,11... | collective-permute-start | bytes 3145736 | tf_op jit(solution)/shard_map/ppermute | solution.py:310

commit v4 on v3

--- a/solution.py
+++ b/solution.py
@@ -44,19 +44,23 @@
 
 
 def hidden_body(n, tiles, parts, down, *refs):
-    dys, ugs, uus = refs[:n], refs[n:2 * n], refs[2 * n:3 * n]
+    dy, dy_more, ugs, uus = refs[0], refs[1:n], refs[n:2 * n], refs[2 * n:3 * n]
     wd, wg_all, wu_all = refs[3 * n:3 * n + 3]
     m = n * parts
-    outs = refs[-(m + 8 + (down > 0) + (down < n)):-(m + 6)]
+    outs = refs[-(m + 8 + n + (down > 0) + (down < n)):-(m + 6 + n)]
     dg, du = outs[:2]
-    ps, (acc, held_g, held_u, wg, wu, sems) = refs[-(m + 6):-6], refs[-6:]
+    ps, (acc, held_g, held_u, wg, wu, sems, dy_sems) = refs[-(m + 6 + n):-(6 + n)], refs[-(6 + n):-n + 1][:6] + (refs[-1],)
+    dys = (dy,) + refs[-n:-1]
+    dy_copies = [pltpu.make_async_copy(a, b, dy_sems.at[k]) for k, (a, b) in enumerate(zip(dy_more, dys[1:]))]
     step = pl.program_id(0)
-    rows = dys[0].shape[0]
+    rows = dy.shape[0]
     piece = rows // parts
 
-    def form(slot):
+    def form(slot, wait=False):
         total = None
         for i in range(n):
+            if wait and i:
+                dy_copies[i - 1].wait()
             span = pl.ds(i * rows, rows)
             grad_h = dot(dys[i][...], wd[...], COLS_T)
             gate = ugs[i][...].astype(F32)
@@ -90,9 +94,9 @@
 
     @pl.when(step == 0)
     def _():
-        for c in fetch(0, 0):
+        for c in dy_copies + fetch(0, 0):
             c.start()
-        form(0)
+        form(0, wait=True)
 
     @pl.when((step > 0) & (step < tiles))
     def _():
@@ -129,13 +133,14 @@
     return pl.pallas_call(
         functools.partial(hidden_body, n, tiles, parts, down),
         grid=(tiles + 1,),
-        in_specs=[once((rows, width))] * n + u_specs + u_specs + [w_now, ANY, ANY] + [ANY] * len(deps),
+        in_specs=[once((rows, width))] + [ANY] * (n - 1) + u_specs + u_specs + [w_now, ANY, ANY] + [ANY] * len(deps),
         out_specs=[tile_out] * 2 + [w_now] * (down > 0) + [z_out] * (down < n) + [once(piece)] * (n * parts),
         out_shape=[wide] * 2 + [jax.ShapeDtypeStruct((cols, width), F32)] * (down > 0)
         + [jax.ShapeDtypeStruct(((n - down) * rows, cols), BF16)] * (down < n)
         + [jax.ShapeDtypeStruct(piece, BF16)] * (n * parts),
         scratch_shapes=[pltpu.VMEM((n * rows, width), F32)] + [pltpu.VMEM((2, n * rows, tile), BF16)] * 2
-        + [pltpu.VMEM((2, width, tile), BF16)] * 2 + [pltpu.SemaphoreType.DMA((2, 2))],
+        + [pltpu.VMEM((2, width, tile), BF16)] * 2 + [pltpu.SemaphoreType.DMA((2, 2))]
+        + [pltpu.VMEM((rows, width), BF16)] * (n - 1) + [pltpu.SemaphoreType.DMA((n - 1,))],
         compiler_params=params(),
         cost_estimate=pl.CostEstimate(flops=(6 * n + 2 * down) * rows * width * cols, bytes_accessed=50 << 20,
                                       transcendentals=n * rows * cols),
@@ -237,13 +242,14 @@
         input_output_aliases={} if prev is None else {6: 1},
         compiler_params=params(24 << 20),
         cost_estimate=pl.CostEstimate(flops=2000 * rows * width, bytes_accessed=14 * rows * width, transcendentals=0),
-    )(*hbm(p_own, p_pair), p_far, *hbm(x_in, grad_res, gamma, *extra))
+    )(*hbm(p_own, p_pair), p_far, *hbm(x_in, grad_res, gamma), *extra)
 
 
 def proj_body(places, tile, more, *refs):
     n = len(places)
     ds, (o, w_out) = refs[:n], refs[n:n + 2]
-    grad_o, grad_w, held, stage, sem_w, sem_o = refs[-6:]
+    grad_o, grad_w, stage, sem_o = refs[-4:] if not more else (refs[-6], refs[-5], refs[-3], refs[-1])
+    held, sem_w = (refs[-4], refs[-2]) if more else (grad_w, None)
     rows = ds[0].shape[0]
     tiles = w_out.shape[1] // tile
     o_rows = [pl.ds(pl.multiple_of(block_of(k) * BLOCK + start, rows), rows) for k, start in places]
@@ -262,14 +268,15 @@
         for i in range(1, n):
             total += dot(o[o_rows[i], :], ds[i][:, cols], ROWS_T)
         held[:, cols] = total + refs[n + 2][:, cols] if more else total
-        w_copy(h).start()
+        if more:
+            w_copy(h).start()
 
     for i in range(n):
         stage[pl.ds(i * rows, rows), :] = dot(ds[i][...], w_out[...], COLS_T).astype(BF16)
         o_copy(i).start()
     for i in range(n):
         o_copy(i).wait()
-    for h in range(tiles):
+    for h in range(tiles if more else 0):
         w_copy(h).wait()
 
 
@@ -283,10 +290,10 @@
     return pl.pallas_call(
         functools.partial(proj_body, [(k, start) for _, k, start in pieces], tile, more),
         in_specs=[vmem] * (n + 2) + ([vmem, ANY] if more else []) + [ANY] * len(deps),
-        out_specs=[ANY, ANY],
+        out_specs=[ANY, ANY if more else vmem],
         out_shape=[jax.ShapeDtypeStruct((tokens, cols), BF16), jax.ShapeDtypeStruct((cols, width), F32)],
-        scratch_shapes=[pltpu.VMEM((cols, width), F32), pltpu.VMEM((n * rows, cols), BF16),
-                        pltpu.SemaphoreType.DMA((width // tile,)), pltpu.SemaphoreType.DMA((n,))],
+        scratch_shapes=([pltpu.VMEM((cols, width), F32)] if more else []) + [pltpu.VMEM((n * rows, cols), BF16)]
+        + ([pltpu.SemaphoreType.DMA((width // tile,))] if more else []) + [pltpu.SemaphoreType.DMA((n,))],
         input_output_aliases={n + 3: 0} if more else {},
         compiler_params=params(16 << 20),
         cost_estimate=pl.CostEstimate(flops=4 * n * rows * width * cols, bytes_accessed=8 << 20, transcendentals=0),
@@ -335,7 +342,7 @@
         x_far = after(x_far, sends[-1])
         x_diag = pair(x_far)
         gw_down = weight_grad([(z_sib, 0), (z_far, 0), (z_far, 1)], [(gy_sib, 0), (gy_far, 0), (gy_diag, 0)],
-                              prev=gw_down, deps=(sends[-1],), tm=512)
+                              prev=gw_down, tm=512)
 
         xs = [(x_norm, 0), (x_sib, 0), (x_far, 0), (x_diag, 0)]
         rest = [functools.partial(weight_grad, xs, [(dg_near, 0), (dg_near, 1), (dg_far, 0), (dg_far, 1)]),
@@ -350,7 +357,7 @@
             places.append(at)
             prev = piece
             if c < len(rest):
-                prev = rest[c](deps=(piece,))
+                prev = rest[c]()
                 grads.append(prev)
             at += n
         gw_gate, gw_up = grads

time: 240 us -> 218 us (0.908)
  waiting for transfers between devices: 50.9 us -> 31.5 us
    ppermute x6, waiting for transfers between devices: 44.2 us -> 24.8 us  [cross(): return lax.ppermute(a, 'tp', CROSS)]
  transfers between devices with their start and end apart: 16 -> 16, of which waited for: 7 -> 7; matrix products, arithmetic and copies ran while one was open for 1% -> 1% of each run, Pallas kernels for 69% -> 75%
where the time goes in v4:
time: 218 us
  Pallas kernels  174 us (80%)
  waiting for transfers between devices  31.5 us (14%)
  starting transfers between devices  10.6 us (5%)
    pallas_call x2, Pallas kernels, hidden(): pl.pallas_call(functools.partial(hidden_body, n, tiles, parts, down), gri...  78.8 us
    pallas_call x3, Pallas kernels, weight_grad(): pl.pallas_call(functools.partial(grad_body if prev is None else grad_more...  70.2 us
    ppermute x6, waiting for transfers between devices, cross(): return lax.ppermute(a, 'tp', CROSS)  24.8 us
    pallas_call x2, Pallas kernels, out_proj(): pl.pallas_call(functools.partial(proj_body, [(k, start) for _, k, start i...  11.4 us
    pallas_call x2, Pallas kernels, norm_backward(): pl.pallas_call(norm_body, grid=(rows // tile,), in_specs=[here, here, rec...  9.29 us
    ppermute x6, starting transfers between devices, cross(): return lax.ppermute(a, 'tp', CROSS)  8.54 us
    ppermute x10, waiting for transfers between devices, pair(): return lax.ppermute(a, 'tp', PAIR)  6.69 us
  transfers between devices with their start and end apart: 16, of which 7 were waited for; matrix products, arithmetic and copies ran while one was open for 1% of the time, Pallas kernels for 75%

profile of v4, /device:TPU:0, one launch (start us, length us, event | category | flops | bytes accessed | tf_op | source)
XLA Modules:
  0.0 217.8 jit_solution(10175576474216473037)
XLA Ops:
  0.6 0.8 collective-permute-start
  1.4 1.3 reshape.15.refs_0_.gamma
  2.7 2.5 %collective-permute-start.2 = (bf16[512,2048]{1,0:T(8,128)(2,1)}, bf16[512,2048]{1,0:T(8,128)(2,1)}, u32[]{:S(2)}, u32[]{:S(2)}) collective-permute-start(bf16[512,2048]{1,0:T(8,128)(2,1)} %refs_0_.3), channel_id=1, source_target_pairs={{0,2},{2,0},{1,3},{3,1},{4,6},{6,4},{5,7},{7,5},{8,10},{10,8},{9,1... | collective-permute-start | bytes 6291464 | tf_op jit(solution)/shard_map/ppermute | solution.py:314
  5.2 0.6 shard_map.163.refs_9_
  5.8 41.7 %shard_map.164 = (bf16[1024,2048]{1,0:T(8,128)(2,1)}, bf16[1024,2048]{1,0:T(8,128)(2,1)}, f32[2048,2048]{1,0:T(8,128)}, bf16[512,2048]{1,0:T(8,128)(2,1)}, bf16[...) custom-call(bf16[512,2048]{1,0:T(8,128)(2,1)} %refs_0_.3, bf16[512,2048]{1,0:T(8,128)(2,1)} %collective-permute-done.refs_1_.refs_3_, ...), custom_call_target="tpu_custom_call" | custom-call | flops 30064771072 | bytes 52428800 | tf_op jit(solution)/shard_map/pallas_call | solution.py:133
  47.5 4.3 %collective-permute-done.2.refs_0_.refs_4_ = bf16[512,2048]{1,0:T(8,128)(2,1)} collective-permute-done((bf16[512,2048]{1,0:T(8,128)(2,1)}, bf16[512,2048]{1,0:T(8,128)(2,1)}, u32[]{:S(2)}, u32[]{:S(2)}) %collective-permute-start.2) | collective-permute-done | bytes 2097184 | tf_op jit(solution)/shard_map/ppermute | solution.py:314
  51.8 1.7 collective-permute-start.7
  53.5 0.6 shard_map.165.refs_9_
  54.1 2.2 collective-permute-done.3.refs_1_.refs_5_
  56.3 37.1 %shard_map.166 = (bf16[1024,2048]{1,0:T(8,128)(2,1)}, bf16[1024,2048]{1,0:T(8,128)(2,1)}, bf16[1024,2048]{1,0:T(8,128)(2,1)}, bf16[256,2048]{1,0:T(8,128)(2,1)},...) custom-call(bf16[512,2048]{1,0:T(8,128)(2,1)} %collective-permute-done.2.refs_0_.refs_4_, ...), custom_call_target="tpu_custom_call" | custom-call | flops 25769803776 | bytes 52428800 | tf_op jit(solution)/shard_map/pallas_call | solution.py:133
  93.4 0.1 collective-permute-start.4
  93.5 0.4 collective-permute-start.9
  93.9 0.1 collective-permute-start.1
  94.0 0.4 collective-permute-start.6
  94.4 1.8 collective-permute-done.4.b
  96.3 1.3 shard_map.167
  97.6 2.5 %collective-permute-done.7.refs_2_ = bf16[512,2048]{1,0:T(8,128)(2,1)} collective-permute-done((bf16[512,2048]{1,0:T(8,128)(2,1)}, bf16[512,2048]{1,0:T(8,128)(2,1)}, u32[]{:S(2)}, u32[]{:S(2)}) %collective-permute-start.7) | collective-permute-done | bytes 2097184 | tf_op jit(solution)/shard_map/ppermute | solution.py:314
  100.1 1.3 shard_map.169
  101.5 1.8 collective-permute-start.10
  103.3 21.5 %shard_map.170 = f32[2048,2048]{1,0:T(8,128)} custom-call(bf16[512,2048]{1,0:T(8,128)(2,1)} %get-tuple-element.44.refs_0_, bf16[1024,2048]{1,0:T(8,128)(2,1)} %get-tuple-element.45.refs_1_.refs_2_, bf16[1024,2048]{1,0:T(8,128)(2,1)} %get-tuple-element.45.refs_1_.refs_2_, ...), custom_call_target="tpu_custom_call", output_to_operand_aliasing={{}: (6, {})} | custom-call | flops 12884901888 | bytes 33554432 | tf_op jit(solution)/shard_map/pallas_call | solution.py:173
  124.8 0.3 collective-permute-start.5
  125.0 2.2 collective-permute-done.10.p_far
  127.2 4.8 %shard_map.171 = (bf16[256,2048]{1,0:T(8,128)(2,1)S(1)}, bf16[512,2048]{1,0:T(8,128)(2,1)}) custom-call(bf16[512,2048]{1,0:T(8,128)(2,1)} %get-tuple-element.33.refs_0_.p_own, bf16[512,2048]{1,0:T(8,128)(2,1)} %collective-permute-done.1.p_pair, bf16[256,2048]{1,0:T(8,128)(2,1)} %collective-permute-done.10.p_far, bf16[512,2048]{1,0:T(8,128)(2,1)} %x_in.3, ...), custom_call_target="tpu_custom_call" | custom-call | flops 1048576000 | bytes 7340032 | tf_op jit(solution)/shard_map/pallas_call | solution.py:236
  132.0 24.3 %shard_map.168 = f32[2048,2048]{1,0:T(8,128)} custom-call(bf16[512,2048]{1,0:T(8,128)(2,1)} %refs_0_.5, bf16[512,2048]{1,0:T(8,128)(2,1)} %collective-permute-done.6.refs_1_, bf16[512,2048]{1,0:T(8,128)(2,1)} %collective-permute-done.7.refs_2_, bf16[512,2048]{1,0:T(8,128)(2,1)} %collective-permute-done.8.refs_3_, ...), custom_call_target="tpu_custom_call" | custom-call | flops 17179869184 | bytes 33554432 | tf_op jit(solution)/shard_map/pallas_call | solution.py:173
  156.3 4.5 %shard_map.172 = (bf16[256,2048]{1,0:T(8,128)(2,1)S(1)}, bf16[512,2048]{1,0:T(8,128)(2,1)}) custom-call(bf16[512,2048]{1,0:T(8,128)(2,1)} %get-tuple-element.33.refs_0_.p_own, bf16[512,2048]{1,0:T(8,128)(2,1)} %collective-permute-done.1.p_pair, bf16[256,2048]{1,0:T(8,128)(2,1)S(1)} %collective-permute-done.5.p_far, ...), custom_call_target="tpu_custom_call", output_to_operand_aliasing={{1}: (6, {})} | custom-call | flops 1048576000 | bytes 7340032 | tf_op jit(solution)/shard_map/pallas_call | solution.py:236
  160.8 2.2 %collective-permute-start.11 = (bf16[256,2048]{1,0:T(8,128)(2,1)S(1)}, bf16[256,2048]{1,0:T(8,128)(2,1)S(1)}, u32[]{:S(2)}, u32[]{:S(2)}) collective-permute-start(bf16[256,2048]{1,0:T(8,128)(2,1)S(1)} %get-tuple-element.50), channel_id=1, source_target_pairs={{0,2},{2,0},{1,3},{3,1},{4,6},{6,4},{5,7},{7,5},{8,10},{10,8},{9,1... | collective-permute-start | bytes 3145736 | tf_op jit(solution)/shard_map/ppermute | solution.py:314
  163.1 24.4 %shard_map.173.refs_4_ = f32[2048,2048]{1,0:T(8,128)} custom-call(bf16[512,2048]{1,0:T(8,128)(2,1)} %refs_0_.5, bf16[512,2048]{1,0:T(8,128)(2,1)} %collective-permute-done.6.refs_1_, bf16[512,2048]{1,0:T(8,128)(2,1)} %collective-permute-done.7.refs_2_, bf16[512,2048]{1,0:T(8,128)(2,1)} %collective-permute-done.8.refs_3_, ...), custom_call_target="tpu_custom_call" | custom-call | flops 17179869184 | bytes 33554432 | tf_op jit(solution)/shard_map/pallas_call | solution.py:173
  187.4 0.2 collective-permute-start.12
  187.7 5.7 %shard_map.174 = (bf16[2048,512]{1,0:T(8,128)(2,1)}, f32[512,2048]{1,0:T(8,128)S(1)}) custom-call(bf16[512,2048]{1,0:T(8,128)(2,1)S(1)} %copy-done, bf16[512,2048]{1,0:T(8,128)(2,1)S(1)} %collective-permute-done.14.refs_1_, bf16[2048,512]{1,0:T(8,128)(2,1)S(1)} %copy-done.1, bf16[512,2048]{1,0:T(8,128)(2,1)S(1)} %copy-done.2, f32[2048,2048]{1,0:T(8,128)} %shard_map.173.refs_4_), custom_call_target="tpu_custom_call" | custom-call | flops 4294967296 | bytes 8388608 | tf_op jit(solution)/shard_map/pallas_call | solution.py:290
  193.4 15.9 %collective-permute-done.13.refs_2_ = bf16[256,2048]{1,0:T(8,128)(2,1)S(1)} collective-permute-done((bf16[256,2048]{1,0:T(8,128)(2,1)S(1)}, bf16[256,2048]{1,0:T(8,128)(2,1)S(1)}, u32[]{:S(2)}, u32[]{:S(2)}) %collective-permute-start.13) | collective-permute-done | bytes 1048608 | tf_op jit(solution)/shard_map/ppermute | solution.py:314
  209.3 2.7 %collective-permute-done.15.refs_3_ = bf16[256,2048]{1,0:T(8,128)(2,1)S(1)} collective-permute-done((bf16[256,2048]{1,0:T(8,128)(2,1)S(1)}, bf16[256,2048]{1,0:T(8,128)(2,1)S(1)}, u32[]{:S(2)}, u32[]{:S(2)}) %collective-permute-start.15) | collective-permute-done | bytes 1048608 | tf_op jit(solution)/shard_map/ppermute | solution.py:317
  212.0 5.7 %shard_map.175 = (bf16[2048,512]{1,0:T(8,128)(2,1)}, f32[512,2048]{1,0:T(8,128)}) custom-call(bf16[256,2048]{1,0:T(8,128)(2,1)S(1)} %collective-permute-done.11.refs_0_, bf16[256,2048]{1,0:T(8,128)(2,1)S(1)} %collective-permute-done.12.refs_1_, bf16[256,2048]{1,0:T(8,128)(2,1)S(1)} %collective-permute-done.13.refs_2_, ...), custom_call_target="tpu_custom_call", output_to_operand_aliasing={{0}: (7, {})} | custom-call | flops 4294967296 | bytes 8388608 | tf_op jit(solution)/shard_map/pallas_call | solution.py:290
  (20 shorter events, 0.1 us)
Async XLA Ops:
  0.6 5.1 %collective-permute-start = (bf16[512,2048]{1,0:T(8,128)(2,1)}, bf16[512,2048]{1,0:T(8,128)(2,1)}, u32[]{:S(2)}, u32[]{:S(2)}) collective-permute-start(bf16[512,2048]{1,0:T(8,128)(2,1)} %refs_0_.3), channel_id=1, source_target_pairs={{0,1},{1,0},{2,3},{3,2},{4,5},{5,4},{6,7},{7,6},{8,9},{9,8},{10,11... | collective-permute-start | bytes 6291464 | tf_op jit(solution)/shard_map/ppermute | solution.py:317
  2.7 49.1 %collective-permute-start.2 = (bf16[512,2048]{1,0:T(8,128)(2,1)}, bf16[512,2048]{1,0:T(8,128)(2,1)}, u32[]{:S(2)}, u32[]{:S(2)}) collective-permute-start(bf16[512,2048]{1,0:T(8,128)(2,1)} %refs_0_.3), channel_id=1, source_target_pairs={{0,2},{2,0},{1,3},{3,1},{4,6},{6,4},{5,7},{7,5},{8,10},{10,8},{9,1... | collective-permute-start | bytes 6291464 | tf_op jit(solution)/shard_map/ppermute | solution.py:314
  51.8 4.5 %collective-permute-start.3 = (bf16[512,2048]{1,0:T(8,128)(2,1)}, bf16[512,2048]{1,0:T(8,128)(2,1)}, u32[]{:S(2)}, u32[]{:S(2)}) collective-permute-start(bf16[512,2048]{1,0:T(8,128)(2,1)} %collective-permute-done.2.refs_0_.refs_4_), channel_id=1, source_target_pairs={{0,1},{1,0},{2,3},{3,2},{4,5},{5,4},{6,7},{7,6},{8,9},{9,8},{10,11... | collective-permute-start | bytes 6291464 | tf_op jit(solution)/shard_map/ppermute | solution.py:317
  51.8 48.4 %collective-permute-start.7 = (bf16[512,2048]{1,0:T(8,128)(2,1)}, bf16[512,2048]{1,0:T(8,128)(2,1)}, u32[]{:S(2)}, u32[]{:S(2)}) collective-permute-start(bf16[512,2048]{1,0:T(8,128)(2,1)} %refs_0_.5), channel_id=1, source_target_pairs={{0,2},{2,0},{1,3},{3,1},{4,6},{6,4},{5,7},{7,5},{8,10},{10,8},{9,1... | collective-permute-start | bytes 6291464 | tf_op jit(solution)/shard_map/ppermute | solution.py:314
  93.4 2.9 %collective-permute-start.4 = (bf16[256,2048]{1,0:T(8,128)(2,1)}, bf16[256,2048]{1,0:T(8,128)(2,1)S(1)}, u32[]{:S(2)}, u32[]{:S(2)}) collective-permute-start(bf16[256,2048]{1,0:T(8,128)(2,1)} %get-tuple-element.37), channel_id=1, source_target_pairs={{0,1},{1,0},{2,3},{3,2},{4,5},{5,4},{6,7},{7,6},{8,9},{9,8},{10,11... | collective-permute-start | bytes 3145736 | tf_op jit(solution)/shard_map/ppermute | solution.py:317
  93.5 6.7 %collective-permute-start.9 = (bf16[256,2048]{1,0:T(8,128)(2,1)}, bf16[256,2048]{1,0:T(8,128)(2,1)S(1)}, u32[]{:S(2)}, u32[]{:S(2)}) collective-permute-start(bf16[256,2048]{1,0:T(8,128)(2,1)} %get-tuple-element.43), channel_id=1, source_target_pairs={{0,1},{1,0},{2,3},{3,2},{4,5},{5,4},{6,7},{7,6},{8,9},{9,8},{10,11... | collective-permute-start | bytes 3145736 | tf_op jit(solution)/shard_map/ppermute | solution.py:317
  93.9 33.3 %collective-permute-start.1 = (bf16[512,2048]{1,0:T(8,128)(2,1)}, bf16[512,2048]{1,0:T(8,128)(2,1)}, u32[]{:S(2)}, u32[]{:S(2)}) collective-permute-start(bf16[512,2048]{1,0:T(8,128)(2,1)} %get-tuple-element.34), channel_id=1, source_target_pairs={{0,1},{1,0},{2,3},{3,2},{4,5},{5,4},{6,7},{7,6},{8,9},{9,8},{10,11... | collective-permute-start | bytes 6291464 | tf_op jit(solution)/shard_map/ppermute | solution.py:317
  94.0 38.1 %collective-permute-start.6 = (bf16[512,2048]{1,0:T(8,128)(2,1)}, bf16[512,2048]{1,0:T(8,128)(2,1)}, u32[]{:S(2)}, u32[]{:S(2)}) collective-permute-start(bf16[512,2048]{1,0:T(8,128)(2,1)} %refs_0_.5), channel_id=1, source_target_pairs={{0,1},{1,0},{2,3},{3,2},{4,5},{5,4},{6,7},{7,6},{8,9},{9,8},{10,11... | collective-permute-start | bytes 6291464 | tf_op jit(solution)/shard_map/ppermute | solution.py:317
  100.1 31.9 %collective-permute-start.8 = (bf16[512,2048]{1,0:T(8,128)(2,1)}, bf16[512,2048]{1,0:T(8,128)(2,1)}, u32[]{:S(2)}, u32[]{:S(2)}) collective-permute-start(bf16[512,2048]{1,0:T(8,128)(2,1)} %collective-permute-done.7.refs_2_), channel_id=1, source_target_pairs={{0,1},{1,0},{2,3},{3,2},{4,5},{5,4},{6,7},{7,6},{8,9},{9,8},{10,11... | collective-permute-start | bytes 6291464 | tf_op jit(solution)/shard_map/ppermute | solution.py:317
  101.5 25.7 %collective-permute-start.10 = (bf16[256,2048]{1,0:T(8,128)(2,1)S(1)}, bf16[256,2048]{1,0:T(8,128)(2,1)}, u32[]{:S(2)}, u32[]{:S(2)}) collective-permute-start(bf16[256,2048]{1,0:T(8,128)(2,1)S(1)} %shard_map.169), channel_id=1, source_target_pairs={{0,2},{2,0},{1,3},{3,1},{4,6},{6,4},{5,7},{7,5},{8,10},{10,8},{9,1... | collective-permute-start | bytes 3145736 | tf_op jit(solution)/shard_map/ppermute | solution.py:314
  124.8 31.6 %collective-permute-start.5 = (bf16[256,2048]{1,0:T(8,128)(2,1)S(1)}, bf16[256,2048]{1,0:T(8,128)(2,1)S(1)}, u32[]{:S(2)}, u32[]{:S(2)}) collective-permute-start(bf16[256,2048]{1,0:T(8,128)(2,1)S(1)} %shard_map.167), channel_id=1, source_target_pairs={{0,2},{2,0},{1,3},{3,1},{4,6},{6,4},{5,7},{7,5},{8,10},{10,8},{9,1... | collective-permute-start | bytes 3145736 | tf_op jit(solution)/shard_map/ppermute | solution.py:314
  160.8 26.9 %collective-permute-start.14 = (bf16[512,2048]{1,0:T(8,128)(2,1)}, bf16[512,2048]{1,0:T(8,128)(2,1)S(1)}, u32[]{:S(2)}, u32[]{:S(2)}) collective-permute-start(bf16[512,2048]{1,0:T(8,128)(2,1)} %get-tuple-element.27.refs_0_), channel_id=1, source_target_pairs={{0,1},{1,0},{2,3},{3,2},{4,5},{5,4},{6,7},{7,6},{8,9},{9,8},{10,11... | collective-permute-start | bytes 6291464 | tf_op jit(solution)/shard_map/ppermute | solution.py:317
  160.8 26.6 %collective-permute-start.11 = (bf16[256,2048]{1,0:T(8,128)(2,1)S(1)}, bf16[256,2048]{1,0:T(8,128)(2,1)S(1)}, u32[]{:S(2)}, u32[]{:S(2)}) collective-permute-start(bf16[256,2048]{1,0:T(8,128)(2,1)S(1)} %get-tuple-element.50), channel_id=1, source_target_pairs={{0,2},{2,0},{1,3},{3,1},{4,6},{6,4},{5,7},{7,5},{8,10},{10,8},{9,1... | collective-permute-start | bytes 3145736 | tf_op jit(solution)/shard_map/ppermute | solution.py:314
  163.0 46.3 %collective-permute-start.13 = (bf16[256,2048]{1,0:T(8,128)(2,1)S(1)}, bf16[256,2048]{1,0:T(8,128)(2,1)S(1)}, u32[]{:S(2)}, u32[]{:S(2)}) collective-permute-start(bf16[256,2048]{1,0:T(8,128)(2,1)S(1)} %get-tuple-element.54), channel_id=1, source_target_pairs={{0,2},{2,0},{1,3},{3,1},{4,6},{6,4},{5,7},{7,5},{8,10},{10,8},{9,1... | collective-permute-start | bytes 3145736 | tf_op jit(solution)/shard_map/ppermute | solution.py:314
  163.0 24.6 %copy-start = (bf16[512,2048]{1,0:T(8,128)(2,1)S(1)}, bf16[512,2048]{1,0:T(8,128)(2,1)}, u32[]{:S(2)}) copy-start(bf16[512,2048]{1,0:T(8,128)(2,1)} %get-tuple-element.27.refs_0_) | copy-start | bytes 6291460
  163.0 24.6 %copy-start.1 = (bf16[2048,512]{1,0:T(8,128)(2,1)S(1)}, bf16[2048,512]{1,0:T(8,128)(2,1)}, u32[]{:S(2)}) copy-start(bf16[2048,512]{1,0:T(8,128)(2,1)} %refs_4_.5) | copy-start | bytes 6291460
  163.0 24.6 %copy-start.2 = (bf16[512,2048]{1,0:T(8,128)(2,1)S(1)}, bf16[512,2048]{1,0:T(8,128)(2,1)}, u32[]{:S(2)}) copy-start(bf16[512,2048]{1,0:T(8,128)(2,1)} %refs_5_.5) | copy-start | bytes 6291460
  187.4 21.9 %collective-permute-start.12 = (bf16[256,2048]{1,0:T(8,128)(2,1)S(1)}, bf16[256,2048]{1,0:T(8,128)(2,1)S(1)}, u32[]{:S(2)}, u32[]{:S(2)}) collective-permute-start(bf16[256,2048]{1,0:T(8,128)(2,1)S(1)} %collective-permute-done.11.refs_0_), channel_id=1, source_target_pairs={{0,1},{1,0},{2,3},{3,2},{4,5},{5,4},{6,7},{7,6},{8,9},{9,8},{10,11... | collective-permute-start | bytes 3145736 | tf_op jit(solution)/shard_map/ppermute | solution.py:317
  209.3 2.7 %collective-permute-start.15 = (bf16[256,2048]{1,0:T(8,128)(2,1)S(1)}, bf16[256,2048]{1,0:T(8,128)(2,1)S(1)}, u32[]{:S(2)}, u32[]{:S(2)}) collective-permute-start(bf16[256,2048]{1,0:T(8,128)(2,1)S(1)} %collective-permute-done.13.refs_2_), channel_id=1, source_target_pairs={{0,1},{1,0},{2,3},{3,2},{4,5},{5,4},{6,7},{7,6},{8,9},{9,8},{10,11... | collective-permute-start | bytes 3145736 | tf_op jit(solution)/shard_map/ppermute | solution.py:317

commit v5 on v4

--- a/solution.py
+++ b/solution.py
@@ -245,11 +245,11 @@
     )(*hbm(p_own, p_pair), p_far, *hbm(x_in, grad_res, gamma), *extra)
 
 
-def proj_body(places, tile, more, *refs):
+def proj_body(places, tile, more, keep, *refs):
     n = len(places)
     ds, (o, w_out) = refs[:n], refs[n:n + 2]
-    grad_o, grad_w, stage, sem_o = refs[-4:] if not more else (refs[-6], refs[-5], refs[-3], refs[-1])
-    held, sem_w = (refs[-4], refs[-2]) if more else (grad_w, None)
+    grad_o, grad_w, stage, sem_o = refs[-4:] if keep else (refs[-6], refs[-5], refs[-3], refs[-1])
+    held, sem_w = (grad_w, None) if keep else (refs[-4], refs[-2])
     rows = ds[0].shape[0]
     tiles = w_out.shape[1] // tile
     o_rows = [pl.ds(pl.multiple_of(block_of(k) * BLOCK + start, rows), rows) for k, start in places]
@@ -268,7 +268,7 @@
         for i in range(1, n):
             total += dot(o[o_rows[i], :], ds[i][:, cols], ROWS_T)
         held[:, cols] = total + refs[n + 2][:, cols] if more else total
-        if more:
+        if not keep:
             w_copy(h).start()
 
     for i in range(n):
@@ -276,11 +276,11 @@
         o_copy(i).start()
     for i in range(n):
         o_copy(i).wait()
-    for h in range(tiles if more else 0):
+    for h in range(0 if keep else tiles):
         w_copy(h).wait()
 
 
-def out_proj(pieces, attn_out, w_out, prev=None, deps=(), tile=1024):
+def out_proj(pieces, attn_out, w_out, prev=None, keep=False, deps=(), tile=1024):
     n = len(pieces)
     tokens, cols = attn_out.shape
     width = w_out.shape[1]
@@ -288,12 +288,12 @@
     vmem = pl.BlockSpec(memory_space=pltpu.VMEM)
     more = prev is not None
     return pl.pallas_call(
-        functools.partial(proj_body, [(k, start) for _, k, start in pieces], tile, more),
+        functools.partial(proj_body, [(k, start) for _, k, start in pieces], tile, more, keep),
         in_specs=[vmem] * (n + 2) + ([vmem, ANY] if more else []) + [ANY] * len(deps),
-        out_specs=[ANY, ANY if more else vmem],
+        out_specs=[ANY, vmem if keep else ANY],
         out_shape=[jax.ShapeDtypeStruct((tokens, cols), BF16), jax.ShapeDtypeStruct((cols, width), F32)],
-        scratch_shapes=([pltpu.VMEM((cols, width), F32)] if more else []) + [pltpu.VMEM((n * rows, cols), BF16)]
-        + ([pltpu.SemaphoreType.DMA((width // tile,))] if more else []) + [pltpu.SemaphoreType.DMA((n,))],
+        scratch_shapes=([] if keep else [pltpu.VMEM((cols, width), F32)]) + [pltpu.VMEM((n * rows, cols), BF16)]
+        + ([] if keep else [pltpu.SemaphoreType.DMA((width // tile,))]) + [pltpu.SemaphoreType.DMA((n,))],
         input_output_aliases={n + 3: 0} if more else {},
         compiler_params=params(16 << 20),
         cost_estimate=pl.CostEstimate(flops=4 * n * rows * width * cols, bytes_accessed=8 << 20, transcendentals=0),
@@ -362,13 +362,14 @@
             at += n
         gw_gate, gw_up = grads
         sib = pair(whole)
-        near = out_proj([(whole, OWN, 0), (sib, SIB, 0)], attn_out, w_out, deps=(gw_up,))
+        near = out_proj([(whole, OWN, 0), (sib, SIB, 0)], attn_out, w_out, keep=True, deps=(gw_up,))
         pieces, prev = [], gw_up
         for c, at in enumerate(places):
             far = after(fars[c], prev)
             pieces += [(far, FAR, at), (pair(far), DIAG, at)]
             prev = near[1]
-        grad_attn, gw_out = out_proj(pieces, attn_out, w_out, near)
+        most = out_proj(pieces[:-1], attn_out, w_out, near, keep=True)
+        grad_attn, gw_out = out_proj(pieces[-1:], attn_out, w_out, most)
         return whole, grad_attn, gw_gate, gw_up, gw_down, gw_out
 
 

time: 218 us -> 217 us (level)
  waiting for transfers between devices: 31.5 us -> 28.8 us
    ppermute x10, waiting for transfers between devices: 6.69 us -> 4.04 us  [pair(): return lax.ppermute(a, 'tp', PAIR)]
    pallas_call x2 -> x3, Pallas kernels: 11.4 us -> 12.8 us  [out_proj(): pl.pallas_call(functools.partial(proj_body, [(k, start) for _, k, start i...]
  transfers between devices with their start and end apart: 16 -> 16, of which waited for: 7 -> 6; matrix products, arithmetic and copies ran while one was open for 1% -> 1% of each run, Pallas kernels for 75% -> 77%
where the time goes in v5:
time: 217 us
  Pallas kernels  175 us (81%)
  waiting for transfers between devices  28.8 us (13%)
  starting transfers between devices  10.6 us (5%)
    pallas_call x2, Pallas kernels, hidden(): pl.pallas_call(functools.partial(hidden_body, n, tiles, parts, down), gri...  78.8 us
    pallas_call x3, Pallas kernels, weight_grad(): pl.pallas_call(functools.partial(grad_body if prev is None else grad_more...  70.2 us
    ppermute x6, waiting for transfers between devices, cross(): return lax.ppermute(a, 'tp', CROSS)  24.8 us
    pallas_call x3, Pallas kernels, out_proj(): pl.pallas_call(functools.partial(proj_body, [(k, start) for _, k, start i...  12.8 us
    pallas_call x2, Pallas kernels, norm_backward(): pl.pallas_call(norm_body, grid=(rows // tile,), in_specs=[here, here, rec...  9.22 us
    ppermute x6, starting transfers between devices, cross(): return lax.ppermute(a, 'tp', CROSS)  8.55 us
  transfers between devices with their start and end apart: 16, of which 6 were waited for; matrix products, arithmetic and copies ran while one was open for 1% of the time, Pallas kernels for 77%

profile of v5, /device:TPU:0, one launch (start us, length us, event | category | flops | bytes accessed | tf_op | source)
XLA Modules:
  0.0 216.6 jit_solution(10009104523960778196)
XLA Ops:
  0.6 0.8 collective-permute-start
  1.4 1.3 reshape.15.refs_0_.gamma
  2.7 2.5 %collective-permute-start.2 = (bf16[512,2048]{1,0:T(8,128)(2,1)}, bf16[512,2048]{1,0:T(8,128)(2,1)}, u32[]{:S(2)}, u32[]{:S(2)}) collective-permute-start(bf16[512,2048]{1,0:T(8,128)(2,1)} %refs_0_.3), channel_id=1, source_target_pairs={{0,2},{2,0},{1,3},{3,1},{4,6},{6,4},{5,7},{7,5},{8,10},{10,8},{9,1... | collective-permute-start | bytes 6291464 | tf_op jit(solution)/shard_map/ppermute | solution.py:314
  5.2 0.6 shard_map.163.refs_9_
  5.8 41.7 %shard_map.164 = (bf16[1024,2048]{1,0:T(8,128)(2,1)}, bf16[1024,2048]{1,0:T(8,128)(2,1)}, f32[2048,2048]{1,0:T(8,128)}, bf16[512,2048]{1,0:T(8,128)(2,1)}, bf16[...) custom-call(bf16[512,2048]{1,0:T(8,128)(2,1)} %refs_0_.3, bf16[512,2048]{1,0:T(8,128)(2,1)} %collective-permute-done.refs_1_.refs_3_, ...), custom_call_target="tpu_custom_call" | custom-call | flops 30064771072 | bytes 52428800 | tf_op jit(solution)/shard_map/pallas_call | solution.py:133
  47.5 4.2 %collective-permute-done.2.refs_0_.refs_4_ = bf16[512,2048]{1,0:T(8,128)(2,1)} collective-permute-done((bf16[512,2048]{1,0:T(8,128)(2,1)}, bf16[512,2048]{1,0:T(8,128)(2,1)}, u32[]{:S(2)}, u32[]{:S(2)}) %collective-permute-start.2) | collective-permute-done | bytes 2097184 | tf_op jit(solution)/shard_map/ppermute | solution.py:314
  51.8 1.7 collective-permute-start.7
  53.5 0.6 shard_map.165.refs_9_
  54.1 2.2 %collective-permute-done.3.refs_1_.refs_5_ = bf16[512,2048]{1,0:T(8,128)(2,1)} collective-permute-done((bf16[512,2048]{1,0:T(8,128)(2,1)}, bf16[512,2048]{1,0:T(8,128)(2,1)}, u32[]{:S(2)}, u32[]{:S(2)}) %collective-permute-start.3) | collective-permute-done | bytes 2097184 | tf_op jit(solution)/shard_map/ppermute | solution.py:317
  56.3 37.1 %shard_map.166 = (bf16[1024,2048]{1,0:T(8,128)(2,1)}, bf16[1024,2048]{1,0:T(8,128)(2,1)}, bf16[1024,2048]{1,0:T(8,128)(2,1)}, bf16[256,2048]{1,0:T(8,128)(2,1)},...) custom-call(bf16[512,2048]{1,0:T(8,128)(2,1)} %collective-permute-done.2.refs_0_.refs_4_, ...), custom_call_target="tpu_custom_call" | custom-call | flops 25769803776 | bytes 52428800 | tf_op jit(solution)/shard_map/pallas_call | solution.py:133
  93.4 0.1 collective-permute-start.4
  93.5 0.4 collective-permute-start.9
  93.9 0.1 collective-permute-start.1
  94.0 0.4 collective-permute-start.6
  94.4 1.8 collective-permute-done.4.b
  96.3 1.3 shard_map.167
  97.6 2.5 %collective-permute-done.7.refs_2_ = bf16[512,2048]{1,0:T(8,128)(2,1)} collective-permute-done((bf16[512,2048]{1,0:T(8,128)(2,1)}, bf16[512,2048]{1,0:T(8,128)(2,1)}, u32[]{:S(2)}, u32[]{:S(2)}) %collective-permute-start.7) | collective-permute-done | bytes 2097184 | tf_op jit(solution)/shard_map/ppermute | solution.py:314
  100.1 1.3 shard_map.169
  101.5 1.8 collective-permute-start.10
  103.3 21.5 %shard_map.170 = f32[2048,2048]{1,0:T(8,128)} custom-call(bf16[512,2048]{1,0:T(8,128)(2,1)} %get-tuple-element.46.refs_0_, bf16[1024,2048]{1,0:T(8,128)(2,1)} %get-tuple-element.47.refs_1_.refs_2_, bf16[1024,2048]{1,0:T(8,128)(2,1)} %get-tuple-element.47.refs_1_.refs_2_, ...), custom_call_target="tpu_custom_call", output_to_operand_aliasing={{}: (6, {})} | custom-call | flops 12884901888 | bytes 33554432 | tf_op jit(solution)/shard_map/pallas_call | solution.py:173
  124.8 0.3 collective-permute-start.5
  125.0 2.2 collective-permute-done.10.p_far
  127.2 4.7 %shard_map.171 = (bf16[256,2048]{1,0:T(8,128)(2,1)S(1)}, bf16[512,2048]{1,0:T(8,128)(2,1)}) custom-call(bf16[512,2048]{1,0:T(8,128)(2,1)} %get-tuple-element.35.refs_0_.p_own, bf16[512,2048]{1,0:T(8,128)(2,1)} %collective-permute-done.1.p_pair, bf16[256,2048]{1,0:T(8,128)(2,1)} %collective-permute-done.10.p_far, bf16[512,2048]{1,0:T(8,128)(2,1)} %x_in.3, ...), custom_call_target="tpu_custom_call" | custom-call | flops 1048576000 | bytes 7340032 | tf_op jit(solution)/shard_map/pallas_call | solution.py:236
  131.9 24.3 %shard_map.168 = f32[2048,2048]{1,0:T(8,128)} custom-call(bf16[512,2048]{1,0:T(8,128)(2,1)} %refs_0_.5, bf16[512,2048]{1,0:T(8,128)(2,1)} %collective-permute-done.6.refs_1_, bf16[512,2048]{1,0:T(8,128)(2,1)} %collective-permute-done.7.refs_2_, bf16[512,2048]{1,0:T(8,128)(2,1)} %collective-permute-done.8.refs_3_, ...), custom_call_target="tpu_custom_call" | custom-call | flops 17179869184 | bytes 33554432 | tf_op jit(solution)/shard_map/pallas_call | solution.py:173
  156.2 4.5 %shard_map.172 = (bf16[256,2048]{1,0:T(8,128)(2,1)S(1)}, bf16[512,2048]{1,0:T(8,128)(2,1)}) custom-call(bf16[512,2048]{1,0:T(8,128)(2,1)} %get-tuple-element.35.refs_0_.p_own, bf16[512,2048]{1,0:T(8,128)(2,1)} %collective-permute-done.1.p_pair, bf16[256,2048]{1,0:T(8,128)(2,1)S(1)} %collective-permute-done.5.p_far, ...), custom_call_target="tpu_custom_call", output_to_operand_aliasing={{1}: (6, {})} | custom-call | flops 1048576000 | bytes 7340032 | tf_op jit(solution)/shard_map/pallas_call | solution.py:236
  160.7 2.2 %collective-permute-start.14 = (bf16[256,2048]{1,0:T(8,128)(2,1)S(1)}, bf16[256,2048]{1,0:T(8,128)(2,1)S(1)}, u32[]{:S(2)}, u32[]{:S(2)}) collective-permute-start(bf16[256,2048]{1,0:T(8,128)(2,1)S(1)} %get-tuple-element.57), channel_id=1, source_target_pairs={{0,2},{2,0},{1,3},{3,1},{4,6},{6,4},{5,7},{7,5},{8,10},{10,8},{9,1... | collective-permute-start | bytes 3145736 | tf_op jit(solution)/shard_map/ppermute | solution.py:314
  163.0 24.4 %shard_map.173.refs_4_ = f32[2048,2048]{1,0:T(8,128)} custom-call(bf16[512,2048]{1,0:T(8,128)(2,1)} %refs_0_.5, bf16[512,2048]{1,0:T(8,128)(2,1)} %collective-permute-done.6.refs_1_, bf16[512,2048]{1,0:T(8,128)(2,1)} %collective-permute-done.7.refs_2_, bf16[512,2048]{1,0:T(8,128)(2,1)} %collective-permute-done.8.refs_3_, ...), custom_call_target="tpu_custom_call" | custom-call | flops 17179869184 | bytes 33554432 | tf_op jit(solution)/shard_map/pallas_call | solution.py:173
  187.4 0.2 collective-permute-start.15
  187.6 5.7 %shard_map.174 = (bf16[2048,512]{1,0:T(8,128)(2,1)}, f32[512,2048]{1,0:T(8,128)S(1)}) custom-call(bf16[512,2048]{1,0:T(8,128)(2,1)S(1)} %copy-done.2, bf16[512,2048]{1,0:T(8,128)(2,1)S(1)} %collective-permute-done.12.refs_1_, bf16[2048,512]{1,0:T(8,128)(2,1)S(1)} %copy-done, bf16[512,2048]{1,0:T(8,128)(2,1)S(1)} %copy-done.1, f32[2048,2048]{1,0:T(8,128)} %shard_map.173.refs_4_), custom_call_target="tpu_custom_call" | custom-call | flops 4294967296 | bytes 8388608 | tf_op jit(solution)/shard_map/pallas_call | solution.py:290
  193.3 15.9 %collective-permute-done.11.refs_2_ = bf16[256,2048]{1,0:T(8,128)(2,1)S(1)} collective-permute-done((bf16[256,2048]{1,0:T(8,128)(2,1)S(1)}, bf16[256,2048]{1,0:T(8,128)(2,1)S(1)}, u32[]{:S(2)}, u32[]{:S(2)}) %collective-permute-start.11) | collective-permute-done | bytes 1048608 | tf_op jit(solution)/shard_map/ppermute | solution.py:314
  209.2 4.6 %shard_map.175 = (bf16[2048,512]{1,0:T(8,128)(2,1)}, f32[512,2048]{1,0:T(8,128)S(1)}) custom-call(bf16[256,2048]{1,0:T(8,128)(2,1)S(1)} %collective-permute-done.14.refs_0_, bf16[256,2048]{1,0:T(8,128)(2,1)S(1)} %collective-permute-done.15.refs_1_, bf16[256,2048]{1,0:T(8,128)(2,1)S(1)} %collective-permute-done.11.refs_2_, ...), custom_call_target="tpu_custom_call", output_to_operand_aliasing={{0}: (6, {})} | custom-call | flops 3221225472 | bytes 8388608 | tf_op jit(solution)/shard_map/pallas_call | solution.py:290
  213.8 2.6 %shard_map.176 = (bf16[2048,512]{1,0:T(8,128)(2,1)}, f32[512,2048]{1,0:T(8,128)}) custom-call(bf16[256,2048]{1,0:T(8,128)(2,1)S(1)} %collective-permute-done.13.refs_0_, bf16[2048,512]{1,0:T(8,128)(2,1)S(1)} %copy-done, bf16[512,2048]{1,0:T(8,128)(2,1)S(1)} %copy-done.1, f32[512,2048]{1,0:T(8,128)S(1)} %get-tuple-element.60.refs_3_, ...), custom_call_target="tpu_custom_call", output_to_operand_aliasing={{0}: (4, {})} | custom-call | flops 1073741824 | bytes 8388608 | tf_op jit(solution)/shard_map/pallas_call | solution.py:290
  (21 shorter events, 0.1 us)
Async XLA Ops:
  0.6 5.1 %collective-permute-start = (bf16[512,2048]{1,0:T(8,128)(2,1)}, bf16[512,2048]{1,0:T(8,128)(2,1)}, u32[]{:S(2)}, u32[]{:S(2)}) collective-permute-start(bf16[512,2048]{1,0:T(8,128)(2,1)} %refs_0_.3), channel_id=1, source_target_pairs={{0,1},{1,0},{2,3},{3,2},{4,5},{5,4},{6,7},{7,6},{8,9},{9,8},{10,11... | collective-permute-start | bytes 6291464 | tf_op jit(solution)/shard_map/ppermute | solution.py:317
  2.7 49.1 %collective-permute-start.2 = (bf16[512,2048]{1,0:T(8,128)(2,1)}, bf16[512,2048]{1,0:T(8,128)(2,1)}, u32[]{:S(2)}, u32[]{:S(2)}) collective-permute-start(bf16[512,2048]{1,0:T(8,128)(2,1)} %refs_0_.3), channel_id=1, source_target_pairs={{0,2},{2,0},{1,3},{3,1},{4,6},{6,4},{5,7},{7,5},{8,10},{10,8},{9,1... | collective-permute-start | bytes 6291464 | tf_op jit(solution)/shard_map/ppermute | solution.py:314
  51.8 4.5 %collective-permute-start.3 = (bf16[512,2048]{1,0:T(8,128)(2,1)}, bf16[512,2048]{1,0:T(8,128)(2,1)}, u32[]{:S(2)}, u32[]{:S(2)}) collective-permute-start(bf16[512,2048]{1,0:T(8,128)(2,1)} %collective-permute-done.2.refs_0_.refs_4_), channel_id=1, source_target_pairs={{0,1},{1,0},{2,3},{3,2},{4,5},{5,4},{6,7},{7,6},{8,9},{9,8},{10,11... | collective-permute-start | bytes 6291464 | tf_op jit(solution)/shard_map/ppermute | solution.py:317
  51.8 48.4 %collective-permute-start.7 = (bf16[512,2048]{1,0:T(8,128)(2,1)}, bf16[512,2048]{1,0:T(8,128)(2,1)}, u32[]{:S(2)}, u32[]{:S(2)}) collective-permute-start(bf16[512,2048]{1,0:T(8,128)(2,1)} %refs_0_.5), channel_id=1, source_target_pairs={{0,2},{2,0},{1,3},{3,1},{4,6},{6,4},{5,7},{7,5},{8,10},{10,8},{9,1... | collective-permute-start | bytes 6291464 | tf_op jit(solution)/shard_map/ppermute | solution.py:314
  93.4 2.9 %collective-permute-start.4 = (bf16[256,2048]{1,0:T(8,128)(2,1)}, bf16[256,2048]{1,0:T(8,128)(2,1)S(1)}, u32[]{:S(2)}, u32[]{:S(2)}) collective-permute-start(bf16[256,2048]{1,0:T(8,128)(2,1)} %get-tuple-element.39), channel_id=1, source_target_pairs={{0,1},{1,0},{2,3},{3,2},{4,5},{5,4},{6,7},{7,6},{8,9},{9,8},{10,11... | collective-permute-start | bytes 3145736 | tf_op jit(solution)/shard_map/ppermute | solution.py:317
  93.5 6.7 %collective-permute-start.9 = (bf16[256,2048]{1,0:T(8,128)(2,1)}, bf16[256,2048]{1,0:T(8,128)(2,1)S(1)}, u32[]{:S(2)}, u32[]{:S(2)}) collective-permute-start(bf16[256,2048]{1,0:T(8,128)(2,1)} %get-tuple-element.45), channel_id=1, source_target_pairs={{0,1},{1,0},{2,3},{3,2},{4,5},{5,4},{6,7},{7,6},{8,9},{9,8},{10,11... | collective-permute-start | bytes 3145736 | tf_op jit(solution)/shard_map/ppermute | solution.py:317
  93.9 33.3 %collective-permute-start.1 = (bf16[512,2048]{1,0:T(8,128)(2,1)}, bf16[512,2048]{1,0:T(8,128)(2,1)}, u32[]{:S(2)}, u32[]{:S(2)}) collective-permute-start(bf16[512,2048]{1,0:T(8,128)(2,1)} %get-tuple-element.36), channel_id=1, source_target_pairs={{0,1},{1,0},{2,3},{3,2},{4,5},{5,4},{6,7},{7,6},{8,9},{9,8},{10,11... | collective-permute-start | bytes 6291464 | tf_op jit(solution)/shard_map/ppermute | solution.py:317
  94.0 37.9 %collective-permute-start.6 = (bf16[512,2048]{1,0:T(8,128)(2,1)}, bf16[512,2048]{1,0:T(8,128)(2,1)}, u32[]{:S(2)}, u32[]{:S(2)}) collective-permute-start(bf16[512,2048]{1,0:T(8,128)(2,1)} %refs_0_.5), channel_id=1, source_target_pairs={{0,1},{1,0},{2,3},{3,2},{4,5},{5,4},{6,7},{7,6},{8,9},{9,8},{10,11... | collective-permute-start | bytes 6291464 | tf_op jit(solution)/shard_map/ppermute | solution.py:317
  100.1 31.8 %collective-permute-start.8 = (bf16[512,2048]{1,0:T(8,128)(2,1)}, bf16[512,2048]{1,0:T(8,128)(2,1)}, u32[]{:S(2)}, u32[]{:S(2)}) collective-permute-start(bf16[512,2048]{1,0:T(8,128)(2,1)} %collective-permute-done.7.refs_2_), channel_id=1, source_target_pairs={{0,1},{1,0},{2,3},{3,2},{4,5},{5,4},{6,7},{7,6},{8,9},{9,8},{10,11... | collective-permute-start | bytes 6291464 | tf_op jit(solution)/shard_map/ppermute | solution.py:317
  101.5 25.7 %collective-permute-start.10 = (bf16[256,2048]{1,0:T(8,128)(2,1)S(1)}, bf16[256,2048]{1,0:T(8,128)(2,1)}, u32[]{:S(2)}, u32[]{:S(2)}) collective-permute-start(bf16[256,2048]{1,0:T(8,128)(2,1)S(1)} %shard_map.169), channel_id=1, source_target_pairs={{0,2},{2,0},{1,3},{3,1},{4,6},{6,4},{5,7},{7,5},{8,10},{10,8},{9,1... | collective-permute-start | bytes 3145736 | tf_op jit(solution)/shard_map/ppermute | solution.py:314
  124.8 31.4 %collective-permute-start.5 = (bf16[256,2048]{1,0:T(8,128)(2,1)S(1)}, bf16[256,2048]{1,0:T(8,128)(2,1)S(1)}, u32[]{:S(2)}, u32[]{:S(2)}) collective-permute-start(bf16[256,2048]{1,0:T(8,128)(2,1)S(1)} %shard_map.167), channel_id=1, source_target_pairs={{0,2},{2,0},{1,3},{3,1},{4,6},{6,4},{5,7},{7,5},{8,10},{10,8},{9,1... | collective-permute-start | bytes 3145736 | tf_op jit(solution)/shard_map/ppermute | solution.py:314
  160.7 26.9 %collective-permute-start.12 = (bf16[512,2048]{1,0:T(8,128)(2,1)}, bf16[512,2048]{1,0:T(8,128)(2,1)S(1)}, u32[]{:S(2)}, u32[]{:S(2)}) collective-permute-start(bf16[512,2048]{1,0:T(8,128)(2,1)} %get-tuple-element.29.refs_0_), channel_id=1, source_target_pairs={{0,1},{1,0},{2,3},{3,2},{4,5},{5,4},{6,7},{7,6},{8,9},{9,8},{10,11... | collective-permute-start | bytes 6291464 | tf_op jit(solution)/shard_map/ppermute | solution.py:317
  160.7 26.6 %collective-permute-start.14 = (bf16[256,2048]{1,0:T(8,128)(2,1)S(1)}, bf16[256,2048]{1,0:T(8,128)(2,1)S(1)}, u32[]{:S(2)}, u32[]{:S(2)}) collective-permute-start(bf16[256,2048]{1,0:T(8,128)(2,1)S(1)} %get-tuple-element.57), channel_id=1, source_target_pairs={{0,2},{2,0},{1,3},{3,1},{4,6},{6,4},{5,7},{7,5},{8,10},{10,8},{9,1... | collective-permute-start | bytes 3145736 | tf_op jit(solution)/shard_map/ppermute | solution.py:314
  162.9 46.3 %collective-permute-start.11 = (bf16[256,2048]{1,0:T(8,128)(2,1)S(1)}, bf16[256,2048]{1,0:T(8,128)(2,1)S(1)}, u32[]{:S(2)}, u32[]{:S(2)}) collective-permute-start(bf16[256,2048]{1,0:T(8,128)(2,1)S(1)} %get-tuple-element.52), channel_id=1, source_target_pairs={{0,2},{2,0},{1,3},{3,1},{4,6},{6,4},{5,7},{7,5},{8,10},{10,8},{9,1... | collective-permute-start | bytes 3145736 | tf_op jit(solution)/shard_map/ppermute | solution.py:314
  163.0 24.6 %copy-start = (bf16[2048,512]{1,0:T(8,128)(2,1)S(1)}, bf16[2048,512]{1,0:T(8,128)(2,1)}, u32[]{:S(2)}) copy-start(bf16[2048,512]{1,0:T(8,128)(2,1)} %refs_1_.1) | copy-start | bytes 6291460
  163.0 24.6 %copy-start.1 = (bf16[512,2048]{1,0:T(8,128)(2,1)S(1)}, bf16[512,2048]{1,0:T(8,128)(2,1)}, u32[]{:S(2)}) copy-start(bf16[512,2048]{1,0:T(8,128)(2,1)} %refs_2_.7) | copy-start | bytes 6291460
  163.0 24.6 %copy-start.2 = (bf16[512,2048]{1,0:T(8,128)(2,1)S(1)}, bf16[512,2048]{1,0:T(8,128)(2,1)}, u32[]{:S(2)}) copy-start(bf16[512,2048]{1,0:T(8,128)(2,1)} %get-tuple-element.29.refs_0_) | copy-start | bytes 6291460
  187.4 21.9 %collective-permute-start.15 = (bf16[256,2048]{1,0:T(8,128)(2,1)S(1)}, bf16[256,2048]{1,0:T(8,128)(2,1)S(1)}, u32[]{:S(2)}, u32[]{:S(2)}) collective-permute-start(bf16[256,2048]{1,0:T(8,128)(2,1)S(1)} %collective-permute-done.14.refs_0_), channel_id=1, source_target_pairs={{0,1},{1,0},{2,3},{3,2},{4,5},{5,4},{6,7},{7,6},{8,9},{9,8},{10,11... | collective-permute-start | bytes 3145736 | tf_op jit(solution)/shard_map/ppermute | solution.py:317
  209.2 4.6 %collective-permute-start.13 = (bf16[256,2048]{1,0:T(8,128)(2,1)S(1)}, bf16[256,2048]{1,0:T(8,128)(2,1)S(1)}, u32[]{:S(2)}, u32[]{:S(2)}) collective-permute-start(bf16[256,2048]{1,0:T(8,128)(2,1)S(1)} %collective-permute-done.11.refs_2_), channel_id=1, source_target_pairs={{0,1},{1,0},{2,3},{3,2},{4,5},{5,4},{6,7},{7,6},{8,9},{9,8},{10,11... | collective-permute-start | bytes 3145736 | tf_op jit(solution)/shard_map/ppermute | solution.py:317
